TPU v7x, 128 devices: a whole 4x4x4 slice. The times are simulated.
128 devices in a mesh: vol: 16 (over y, z), pix: 8 (over x, core).
Axes of the slice: x: 4, y: 4, z: 4, core: 2. Of those that a mesh axis runs over, the one named last changes fastest.
Arguments:
- kernel: bfloat16 [2097152, 128], P(('vol', 'pix')), may hold values from 0 to 0.25
- pressure: bfloat16 [2097152], P(('vol', 'pix')), may hold values from 0.049804688 to 2
- velocity: bfloat16 [2097152], P(('vol', 'pix')), may hold values from -4 to 4
- entry_slot: int32 [128, 16384], P(('vol', 'pix')), may hold values from 0 to 1023, never falling along the last dimension, each value on 1 to 32 neighbouring positions
- slot_tile: int32 [128, 1024], P(('vol', 'pix')), may hold values from 0 to 32767, as said below
- tile_owner: int32 [32768], replicated, may hold values from 0 to 7, as said below
Outputs:
- owned_tiles: float32 [65536, 256], P(('vol', 'pix'))
- shell_map: float32 [32768, 256], P('vol')
Inputs may be any that keep to these rules, and one draw needn't show every extreme that they name: `entry_slot`: for each device the slot numbers never fall along its 16384 crossings; every slot has at least one crossing and at most 32. `tile_owner`: within every block of 2048 consecutive tiles each pix index owns 256 // 2 to 512 tiles, and one owner of each block owns exactly 512. `slot_tile`: the 1024 tiles of one device are distinct; at most 16 of them belong to any one owning device (vol index t // 2048, pix index tile_owner[t]), and one owning device gets exactly 16 from every device.
All inputs are finite; a program needn't handle non-finite values.
Results may differ from a plain program's by a relative error of at most 0.0003.
Values sent between devices are 32-bit elements; how exact they have to be, the bound alone decides.
A program may use at most 64 MiB of HBM per device.

v0:
```python
import jax
import jax.numpy as jnp
from jax import lax
from jax.sharding import PartitionSpec as P


def split_up(value, dim, size):
    shape = value.shape
    blocks = value.reshape(*shape[:dim], size, shape[dim] // size, *shape[dim + 1 :])
    return jnp.moveaxis(blocks, dim, 0)


def joined_along(blocks, dim):
    shape = list(blocks.shape[1:])
    shape[dim] *= blocks.shape[0]
    return jnp.moveaxis(blocks, 0, dim).reshape(shape)


def joined_exchange(value, axis, axes, splits, concats):
    sizes = [lax.axis_size(a) for a in axes]
    blocks = split_up(value, splits[0], sizes[0])
    blocks = jnp.moveaxis(split_up(blocks, splits[1] + 1, sizes[1]), 0, 1)
    inside = blocks.shape[2:]
    blocks = blocks.reshape(-1, *inside)
    blocks = lax.all_to_all(blocks, axis, split_axis=0, concat_axis=0, tiled=True)
    blocks = joined_along(blocks.reshape(*sizes, *inside), concats[0] + 1)
    return joined_along(blocks, concats[1])


def project(kernel, pressure, velocity, entry_slot, slot_count):
    entry_count = kernel.shape[0]
    pixel_count = kernel.shape[1]
    block_rows = min(256, entry_count)
    block_count = entry_count // block_rows
    turn_count = min(16, block_count)
    group_size = block_count // turn_count
    within = jnp.arange(block_rows, dtype=jnp.int32)
    nothing = jnp.zeros((), kernel.dtype)

    def accumulate(running, inputs):
        kernel_weights, thermal, kinetic, slot_ids = inputs
        offsets = slot_ids[:, 0]
        local_slot = slot_ids - offsets[:, None]
        matches = within[None, :, None] == local_slot[:, None, :]
        particle_weights = jnp.stack(
            [
                jnp.where(matches, thermal[:, None, :], nothing),
                jnp.where(matches, kinetic[:, None, :], nothing),
            ],
            axis=2,
        )
        particle_weights = particle_weights.reshape(group_size, 2 * block_rows, block_rows)
        pixel_products = jnp.einsum(
            "vzc,vcx->vzx", particle_weights, kernel_weights, preferred_element_type=jnp.float32
        )
        pixel_products = pixel_products.reshape(group_size * block_rows, 2 * pixel_count)
        target_rows = (offsets[:, None] + within[None, :]).reshape(group_size * block_rows)
        return (running.at[target_rows].add(pixel_products), None)

    start_value = jnp.zeros((slot_count + block_rows, 2 * pixel_count), jnp.float32)
    inputs = (
        kernel.reshape(turn_count, group_size, block_rows, pixel_count),
        pressure.reshape(turn_count, group_size, block_rows),
        velocity.reshape(turn_count, group_size, block_rows),
        entry_slot.reshape(turn_count, group_size, block_rows),
    )
    result, unused = lax.scan(accumulate, start_value, inputs)
    return result[:slot_count]


def owner_rows(tile_owner, vol_count, pix_count):
    tile_count = tile_owner.shape[0]
    owners = tile_owner.reshape(vol_count, tile_count // vol_count)
    matches = owners[:, None, :] == jnp.arange(pix_count, dtype=jnp.int32)[None, :, None]
    owner_ranking = jnp.cumsum(matches.astype(jnp.int32), axis=2, dtype=jnp.int32) - 1
    return jnp.sum(jnp.where(matches, owner_ranking, 0), axis=1, dtype=jnp.int32).reshape(
        tile_count
    )


def shards(kernel, pressure, velocity, entry_slot, slot_tile, tile_owner):
    vol_count = lax.axis_size("vol")
    pix_count = lax.axis_size("pix")
    device_count = vol_count * pix_count
    slot_count = slot_tile.shape[1]
    tile_count = tile_owner.shape[0]
    block_tile_list = tile_count // vol_count
    owned_most = 2 * block_tile_list // pix_count
    bucket_size = 2 * slot_count // device_count
    partial_value = project(kernel, pressure, velocity, entry_slot[0], slot_count)
    tile_width = partial_value.shape[1]
    row_of_tile = owner_rows(tile_owner, vol_count, pix_count)
    targets = slot_tile[0]
    target_dev = targets // block_tile_list * pix_count + tile_owner[targets]
    target_row = row_of_tile[targets]
    labels = jnp.arange(device_count, dtype=jnp.int32)
    matches = labels[:, None] == target_dev[None, :]
    owner_ranking = jnp.cumsum(matches.astype(jnp.int32), axis=1, dtype=jnp.int32) - 1
    position = jnp.sum(jnp.where(matches, owner_ranking, 0), axis=0, dtype=jnp.int32)
    bucket = target_dev * bucket_size + position
    outgoing = (
        jnp.zeros((device_count * bucket_size, tile_width), jnp.float32)
        .at[bucket]
        .set(partial_value)
    )
    destined = (
        jnp.full((device_count * bucket_size,), owned_most, jnp.int32).at[bucket].set(target_row)
    )
    arrived, arrived_rows = (
        joined_exchange(
            outgoing.reshape(vol_count, pix_count, bucket_size, tile_width),
            ("vol", "pix"),
            ("vol", "pix"),
            (0, 1),
            (0, 1),
        ),
        joined_exchange(
            destined.reshape(vol_count, pix_count, bucket_size),
            ("vol", "pix"),
            ("vol", "pix"),
            (0, 1),
            (0, 1),
        ),
    )
    owned = jax.ops.segment_sum(
        arrived.reshape(-1, tile_width), arrived_rows.reshape(-1), num_segments=owned_most + 1
    )[:owned_most]
    volume_index = lax.axis_index("vol")
    block_owner = lax.dynamic_slice_in_dim(
        tile_owner, volume_index * block_tile_list, block_tile_list
    )
    block_row = lax.dynamic_slice_in_dim(
        row_of_tile, volume_index * block_tile_list, block_tile_list
    )
    source = block_owner * owned_most + block_row
    gathered_piece = lax.all_gather(owned, "pix", axis=0, tiled=True)
    piece_rows = gathered_piece.shape[0]
    inside = (source >= 0) & (source < piece_rows)
    taken = gathered_piece[jnp.clip(source, 0, piece_rows - 1)]
    shell_map = jnp.where(inside[:, None], taken, 0.0)
    return (owned, shell_map)


def solution(mesh):
    in_specs = (
        P(("vol", "pix"), None),
        P(("vol", "pix")),
        P(("vol", "pix")),
        P(("vol", "pix"), None),
        P(("vol", "pix"), None),
        P(),
    )
    out_specs = (P(("vol", "pix"), None), P("vol", None))
    return jax.shard_map(shards, mesh=mesh, in_specs=in_specs, out_specs=out_specs, check_vma=False)
```

profile of v0, /device:TPU:1, one launch (start us, length us, event | category | flops | bytes accessed | tf_op | source)
XLA Modules:
  0.0 449.3 jit_solution(6311046077614405091)
XLA Ops:
  16.9 36.3 %reduce-window.16 = s32[16,8,16,128]{3,2,1,0:T(8,128)S(1)} reduce-window(s32[16,8,16,128]{3,2,1,0:T(8,128)S(1)} %fusion.10, s32[]{:T(128)} %constant.36.clone.1), window={size=1x1x1x128 pad=0_0x0_0x0_0x127_0}, to_apply=%region_3.4 | reduce-window | flops 33292288 | bytes 2097156 | tf_op jit(solution)/shard_map/reduce-window.2
  70.0 11.5 %all-to-all-start = ((s32[128,1,1,16]{3,2,1,0:T(1,128)}), s32[128,1,1,16]{3,2,1,0:T(1,128)S(1)}, u32[]{:S(2)}, u32[]{:S(2)}) async-start(s32[128,1,1,16]{3,2,1,0:T(1,128)} %bitcast.10), calls=%async_computation | async-start | bytes 131072 | tf_op jit(solution)/shard_map/all_to_all | solution.py:25
  83.0 261.3 %while.12 = (s32[]{:T(128)}, f32[1280,256]{1,0:T(8,128)S(1)}, s32[16,4,256]{2,1,0:T(4,128)S(1)}, bf16[16,4,256]{2,1,0:T(4,128)(2,1)S(1)}, bf16[16,4,256]{2,1,0:T...) while((s32[]{:T(128)}, f32[1280,256]{1,0:T(8,128)S(1)}, ...), condition=%wide.region_9.10_spmd.clone.clone, body=%wide.region_7.9_spmd.clone.clone.sunk | while | flops 137368576 | bytes 12902549 | solution.py:67
  92.8 6.5 %scatter_fusion = f32[1280,256]{1,0:T(8,128)S(1)} fusion(f32[1280,256]{1,0:T(8,128)S(1)} %get-tuple-element.150, s32[1024]{0:T(1024)S(1)} %bitcast.88, f32[1024,256]{1,0:T(8,128)S(1)} %reshape.366), kind=kCustom, calls=%fused_computation.3.clone.clone.1 | custom fusion | flops 262144 | bytes 3149824 | tf_op jit(solution)/shard_map/while/body/eval_jaxpr/scatter-add | solution.py:58
  109.1 6.5 %scatter_fusion = f32[1280,256]{1,0:T(8,128)S(1)} fusion(f32[1280,256]{1,0:T(8,128)S(1)} %get-tuple-element.150, s32[1024]{0:T(1024)S(1)} %bitcast.88, f32[1024,256]{1,0:T(8,128)S(1)} %reshape.366), kind=kCustom, calls=%fused_computation.3.clone.clone.1 | custom fusion | flops 262144 | bytes 3149824 | tf_op jit(solution)/shard_map/while/body/eval_jaxpr/scatter-add | solution.py:58
  125.4 6.5 %scatter_fusion = f32[1280,256]{1,0:T(8,128)S(1)} fusion(f32[1280,256]{1,0:T(8,128)S(1)} %get-tuple-element.150, s32[1024]{0:T(1024)S(1)} %bitcast.88, f32[1024,256]{1,0:T(8,128)S(1)} %reshape.366), kind=kCustom, calls=%fused_computation.3.clone.clone.1 | custom fusion | flops 262144 | bytes 3149824 | tf_op jit(solution)/shard_map/while/body/eval_jaxpr/scatter-add | solution.py:58
  141.8 6.5 %scatter_fusion = f32[1280,256]{1,0:T(8,128)S(1)} fusion(f32[1280,256]{1,0:T(8,128)S(1)} %get-tuple-element.150, s32[1024]{0:T(1024)S(1)} %bitcast.88, f32[1024,256]{1,0:T(8,128)S(1)} %reshape.366), kind=kCustom, calls=%fused_computation.3.clone.clone.1 | custom fusion | flops 262144 | bytes 3149824 | tf_op jit(solution)/shard_map/while/body/eval_jaxpr/scatter-add | solution.py:58
  158.1 6.5 %scatter_fusion = f32[1280,256]{1,0:T(8,128)S(1)} fusion(f32[1280,256]{1,0:T(8,128)S(1)} %get-tuple-element.150, s32[1024]{0:T(1024)S(1)} %bitcast.88, f32[1024,256]{1,0:T(8,128)S(1)} %reshape.366), kind=kCustom, calls=%fused_computation.3.clone.clone.1 | custom fusion | flops 262144 | bytes 3149824 | tf_op jit(solution)/shard_map/while/body/eval_jaxpr/scatter-add | solution.py:58
  174.4 6.5 %scatter_fusion = f32[1280,256]{1,0:T(8,128)S(1)} fusion(f32[1280,256]{1,0:T(8,128)S(1)} %get-tuple-element.150, s32[1024]{0:T(1024)S(1)} %bitcast.88, f32[1024,256]{1,0:T(8,128)S(1)} %reshape.366), kind=kCustom, calls=%fused_computation.3.clone.clone.1 | custom fusion | flops 262144 | bytes 3149824 | tf_op jit(solution)/shard_map/while/body/eval_jaxpr/scatter-add | solution.py:58
  190.8 6.5 %scatter_fusion = f32[1280,256]{1,0:T(8,128)S(1)} fusion(f32[1280,256]{1,0:T(8,128)S(1)} %get-tuple-element.150, s32[1024]{0:T(1024)S(1)} %bitcast.88, f32[1024,256]{1,0:T(8,128)S(1)} %reshape.366), kind=kCustom, calls=%fused_computation.3.clone.clone.1 | custom fusion | flops 262144 | bytes 3149824 | tf_op jit(solution)/shard_map/while/body/eval_jaxpr/scatter-add | solution.py:58
  207.1 6.5 %scatter_fusion = f32[1280,256]{1,0:T(8,128)S(1)} fusion(f32[1280,256]{1,0:T(8,128)S(1)} %get-tuple-element.150, s32[1024]{0:T(1024)S(1)} %bitcast.88, f32[1024,256]{1,0:T(8,128)S(1)} %reshape.366), kind=kCustom, calls=%fused_computation.3.clone.clone.1 | custom fusion | flops 262144 | bytes 3149824 | tf_op jit(solution)/shard_map/while/body/eval_jaxpr/scatter-add | solution.py:58
  223.4 6.5 %scatter_fusion = f32[1280,256]{1,0:T(8,128)S(1)} fusion(f32[1280,256]{1,0:T(8,128)S(1)} %get-tuple-element.150, s32[1024]{0:T(1024)S(1)} %bitcast.88, f32[1024,256]{1,0:T(8,128)S(1)} %reshape.366), kind=kCustom, calls=%fused_computation.3.clone.clone.1 | custom fusion | flops 262144 | bytes 3149824 | tf_op jit(solution)/shard_map/while/body/eval_jaxpr/scatter-add | solution.py:58
  239.8 6.5 %scatter_fusion = f32[1280,256]{1,0:T(8,128)S(1)} fusion(f32[1280,256]{1,0:T(8,128)S(1)} %get-tuple-element.150, s32[1024]{0:T(1024)S(1)} %bitcast.88, f32[1024,256]{1,0:T(8,128)S(1)} %reshape.366), kind=kCustom, calls=%fused_computation.3.clone.clone.1 | custom fusion | flops 262144 | bytes 3149824 | tf_op jit(solution)/shard_map/while/body/eval_jaxpr/scatter-add | solution.py:58
  256.1 6.5 %scatter_fusion = f32[1280,256]{1,0:T(8,128)S(1)} fusion(f32[1280,256]{1,0:T(8,128)S(1)} %get-tuple-element.150, s32[1024]{0:T(1024)S(1)} %bitcast.88, f32[1024,256]{1,0:T(8,128)S(1)} %reshape.366), kind=kCustom, calls=%fused_computation.3.clone.clone.1 | custom fusion | flops 262144 | bytes 3149824 | tf_op jit(solution)/shard_map/while/body/eval_jaxpr/scatter-add | solution.py:58
  272.4 6.5 %scatter_fusion = f32[1280,256]{1,0:T(8,128)S(1)} fusion(f32[1280,256]{1,0:T(8,128)S(1)} %get-tuple-element.150, s32[1024]{0:T(1024)S(1)} %bitcast.88, f32[1024,256]{1,0:T(8,128)S(1)} %reshape.366), kind=kCustom, calls=%fused_computation.3.clone.clone.1 | custom fusion | flops 262144 | bytes 3149824 | tf_op jit(solution)/shard_map/while/body/eval_jaxpr/scatter-add | solution.py:58
  288.8 6.5 %scatter_fusion = f32[1280,256]{1,0:T(8,128)S(1)} fusion(f32[1280,256]{1,0:T(8,128)S(1)} %get-tuple-element.150, s32[1024]{0:T(1024)S(1)} %bitcast.88, f32[1024,256]{1,0:T(8,128)S(1)} %reshape.366), kind=kCustom, calls=%fused_computation.3.clone.clone.1 | custom fusion | flops 262144 | bytes 3149824 | tf_op jit(solution)/shard_map/while/body/eval_jaxpr/scatter-add | solution.py:58
  305.1 6.5 %scatter_fusion = f32[1280,256]{1,0:T(8,128)S(1)} fusion(f32[1280,256]{1,0:T(8,128)S(1)} %get-tuple-element.150, s32[1024]{0:T(1024)S(1)} %bitcast.88, f32[1024,256]{1,0:T(8,128)S(1)} %reshape.366), kind=kCustom, calls=%fused_computation.3.clone.clone.1 | custom fusion | flops 262144 | bytes 3149824 | tf_op jit(solution)/shard_map/while/body/eval_jaxpr/scatter-add | solution.py:58
  321.4 6.5 %scatter_fusion = f32[1280,256]{1,0:T(8,128)S(1)} fusion(f32[1280,256]{1,0:T(8,128)S(1)} %get-tuple-element.150, s32[1024]{0:T(1024)S(1)} %bitcast.88, f32[1024,256]{1,0:T(8,128)S(1)} %reshape.366), kind=kCustom, calls=%fused_computation.3.clone.clone.1 | custom fusion | flops 262144 | bytes 3149824 | tf_op jit(solution)/shard_map/while/body/eval_jaxpr/scatter-add | solution.py:58
  337.8 6.5 %scatter_fusion = f32[1280,256]{1,0:T(8,128)S(1)} fusion(f32[1280,256]{1,0:T(8,128)S(1)} %get-tuple-element.150, s32[1024]{0:T(1024)S(1)} %bitcast.88, f32[1024,256]{1,0:T(8,128)S(1)} %reshape.366), kind=kCustom, calls=%fused_computation.3.clone.clone.1 | custom fusion | flops 262144 | bytes 3149824 | tf_op jit(solution)/shard_map/while/body/eval_jaxpr/scatter-add | solution.py:58
  350.6 9.8 %all-to-all-start.1 = ((f32[128,1,1,16,256]{4,3,2,1,0:T(8,128)}), f32[128,1,1,16,256]{4,3,2,1,0:T(8,128)S(1)}, u32[]{:S(2)}, u32[]{:S(2)}) async-start(f32[128,1,1,16,256]{4,3,2,1,0:T(8,128)} %bitcast.86), calls=%async_computation.1 | async-start | bytes 4194304 | tf_op jit(solution)/shard_map/all_to_all | solution.py:25
  360.7 30.1 %all-to-all-done.1 = f32[128,1,1,16,256]{4,3,2,1,0:T(8,128)S(1)} async-done(((f32[128,1,1,16,256]{4,3,2,1,0:T(8,128)}), f32[128,1,1,16,256]{4,3,2,1,0:T(8,128)S(1)}, u32[]{:S(2)}, u32[]{:S(2)}) %all-to-all-start.1) | async-done | bytes 2097184 | tf_op jit(solution)/shard_map/all_to_all | solution.py:25
  390.8 11.7 %scatter_custom_fusion.3 = f32[513,256]{1,0:T(8,128)S(1)} fusion(s32[2048]{0:T(1024)S(1)} %reshape.329, f32[2048,256]{1,0:T(8,128)S(1)} %bitcast.87, f32[]{:T(128)} %constant.26.clone.1), kind=kCustom, calls=%fused_computation.35 | custom fusion | flops 524288 | bytes 525316 | tf_op jit(solution)/shard_map/scatter-add | solution.py:125
  403.4 28.6 %all-gather.2.cloned.1.call-done = f32[4096,256]{1,0:T(8,128)} async-done(((f32[512,256]{1,0:T(8,128)}), f32[4096,256]{1,0:T(8,128)}) %all-gather.2.cloned.1.call-update) | async-done | bytes 4194320 | tf_op jit(solution)/shard_map/all_gather | solution.py:136
  432.0 8.8 %gather_fusion.2 = f32[2048,256]{1,0:T(8,128)S(1)} fusion(f32[4096,256]{1,0:T(8,128)} %all-gather.2.cloned.1.call-done, s32[2048]{0:T(1024)S(1)} %fusion.16), kind=kCustom, calls=%fused_computation.2 | custom fusion | bytes 4202496 | tf_op jit(solution)/shard_map/gather | solution.py:139
  (220 shorter events, 192.6 us)
Async XLA Ops:
  7.9 6.0 %copy-start.2 = (s32[1,1024]{1,0:T(1,128)S(1)}, s32[1,1024]{1,0:T(1,128)}, u32[]{:S(2)}) copy-start(s32[1,1024]{1,0:T(1,128)} %param.12) | copy-start | bytes 12292
  7.9 8.9 %copy-start = (s32[32768]{0:T(1024)S(1)}, s32[32768]{0:T(1024)}, u32[]{:S(2)}) copy-start(s32[32768]{0:T(1024)} %param.13) | copy-start | bytes 393220
  58.7 22.8 %copy-start.3 = (bf16[16384]{0:T(1024)(128)(2,1)S(1)}, bf16[16384]{0:T(1024)(128)(2,1)}, u32[]{:S(2)}) copy-start(bf16[16384]{0:T(1024)(128)(2,1)} %param.9) | copy-start | bytes 98308
  58.7 22.8 %copy-start.4 = (bf16[16384]{0:T(1024)(128)(2,1)S(1)}, bf16[16384]{0:T(1024)(128)(2,1)}, u32[]{:S(2)}) copy-start(bf16[16384]{0:T(1024)(128)(2,1)} %param.10) | copy-start | bytes 98308
  58.7 23.4 %copy-start.1 = (s32[1,16384]{1,0:T(1,128)S(1)}, s32[1,16384]{1,0:T(1,128)}, u32[]{:S(2)}) copy-start(s32[1,16384]{1,0:T(1,128)} %param.11) | copy-start | bytes 196612
  70.0 280.6 %all-to-all-start = ((s32[128,1,1,16]{3,2,1,0:T(1,128)}), s32[128,1,1,16]{3,2,1,0:T(1,128)S(1)}, u32[]{:S(2)}, u32[]{:S(2)}) async-start(s32[128,1,1,16]{3,2,1,0:T(1,128)} %bitcast.10), calls=%async_computation | async-start | bytes 131072 | tf_op jit(solution)/shard_map/all_to_all | solution.py:25
  350.6 40.2 %all-to-all-start.1 = ((f32[128,1,1,16,256]{4,3,2,1,0:T(8,128)}), f32[128,1,1,16,256]{4,3,2,1,0:T(8,128)S(1)}, u32[]{:S(2)}, u32[]{:S(2)}) async-start(f32[128,1,1,16,256]{4,3,2,1,0:T(8,128)} %bitcast.86), calls=%async_computation.1 | async-start | bytes 4194304 | tf_op jit(solution)/shard_map/all_to_all | solution.py:25
  360.4 71.6 %all-gather.2.cloned.1.call-start = ((), (), s32[]{:S(2)}) async-start(), calls=%async_computation.2 | async-start | bytes 4718592 | tf_op jit(solution)/shard_map/all_gather | solution.py:136
Sparse Core Ops, SparseCore 0:
  403.5 28.4 all-gather.1
where the time goes:
time: 451 us; the launch traced here: 449 us
  other arithmetic  228 us (51%)
  local copies, waits for them, and re-layouts  82.9 us (18%)
  waiting for transfers between devices  58.7 us (13%)
  matrix products  43.1 us (10%)
  starting transfers between devices  21.5 us (5%)
  between operations  14.3 us (3%)
    scatter-add x16, other arithmetic, accumulate(): return (running.at[target_rows].add(pixel_products), None)  105 us
    dot_general x16, matrix products, accumulate(): jnp.einsum('vzc,vcx->vzx', particle_weights, kernel_weights, preferred_el...  43.1 us
    another operation x4, other arithmetic  39.2 us
    another operation x16, other arithmetic, accumulate(): jnp.stack([jnp.where(matches, thermal[:, None, :], nothing), jnp.where(ma...  38.9 us
    all_to_all x2, waiting for transfers between devices, joined_exchange(): lax.all_to_all(blocks, axis, split_axis=0, concat_axis=0, tiled=True)  30.1 us
    all_gather x1, waiting for transfers between devices, shards(): gathered_piece = lax.all_gather(owned, 'pix', axis=0, tiled=True)  28.6 us
    select_n x16, other arithmetic, accumulate(): jnp.where(matches, thermal[:, None, :], nothing)  25.9 us
    reshape x16, local copies, waits for them, and re-layouts, accumulate(): pixel_products.reshape(group_size * block_rows, 2 * pixel_count)  24.6 us
  transfers between devices with their start and end apart: 3, of which 2 were waited for; matrix products, arithmetic and copies ran while one was open for 60% of the time, Pallas kernels for 0%

commit v1 on v0

v1 whole, which is shorter than its diff:
```python
import functools

import jax
import jax.numpy as jnp
from jax import lax
from jax.experimental import pallas as pl
from jax.experimental.pallas import tpu as pltpu
from jax.sharding import PartitionSpec as P

MESH = pl.DeviceIdType.MESH
F32 = jnp.float32
BF16 = jnp.bfloat16

LANES = 128
ENTRIES = 16384
SLOTS = 1024
N_VOL = 16
SIDE = 4
BLOCK_TILES = 2048
CAP = 128
OWN_MAX = 512

STEP = 2048
SPAN = 256
WINDOW = 32
MSG = 2 * CAP + 8
FIRST = CAP + 8


def dot(a, b):
    return jnp.dot(a, b, preferred_element_type=F32)


def iota(shape, dim):
    return lax.broadcasted_iota(jnp.int32, shape, dim)


def halves(x):
    high = x.astype(BF16)
    return high, (x - high.astype(F32)).astype(BF16)


def project_kernel(slot_s, kernel_ref, pressure_ref, velocity_ref, slot_ref, tile_ref, send_ref, acc, rhs):
    step = pl.program_id(0)

    @pl.when(step == 0)
    def _():
        acc[...] = jnp.zeros_like(acc)

    thermal = pressure_ref[...].astype(F32)
    kinetic = velocity_ref[...].astype(F32)
    slots = slot_ref[...]
    rows = iota((WINDOW, LANES), 0)

    def products(i, base):
        top, low = [], []
        for h in range(SPAN // LANES):
            r = i * (SPAN // LANES) + h
            match = rows == slots[r : r + 1, :] - base
            top.append(jnp.where(match, thermal[r : r + 1, :], 0.0))
            low.append(jnp.where(match, kinetic[r : r + 1, :], 0.0))
        weights = jnp.concatenate([jnp.concatenate(top, 1), jnp.concatenate(low, 1)], 0)
        return dot(weights.astype(BF16), kernel_ref[i * SPAN : (i + 1) * SPAN, :])

    def add(base, value):
        acc[0, pl.ds(base, WINDOW), :] += value[:WINDOW]
        acc[1, pl.ds(base, WINDOW), :] += value[WINDOW:]

    bases, lasts, values = [], [], []
    for i in range(STEP // SPAN):
        r = i * (SPAN // LANES)
        bases.append(pl.multiple_of((slot_s[r, 0] // 8) * 8, 8))
        lasts.append(slot_s[r + SPAN // LANES - 1, LANES - 1])
        values.append(products(i, bases[i]))
    for i in range(STEP // SPAN):
        add(bases[i], values[i])
    for i in range(STEP // SPAN):

        @pl.loop(1, (lasts[i] - bases[i]) // WINDOW + 1)
        def _(w, i=i):
            base = pl.multiple_of(bases[i] + w * WINDOW, 8)
            add(base, products(i, base))

    @pl.when(step == pl.num_programs(0) - 1)
    def _():
        tiles = tile_ref[...]
        block = tiles // BLOCK_TILES
        within = tiles - block * BLOCK_TILES
        groups = SLOTS // LANES
        match = jnp.concatenate([(block == v).astype(F32) for v in range(N_VOL)], 0).astype(BF16)
        r, c = iota((LANES, LANES), 0), iota((LANES, LANES), 1)
        before = (r < c).astype(F32).astype(BF16)
        above = ((c < r) & (c // groups == r // groups)).astype(F32).astype(BF16)
        ones = jnp.ones((LANES, LANES), BF16)
        rank = dot(match, before) + dot(dot(above, match).astype(BF16), ones)
        key = jnp.where(match.astype(F32) > 0, rank, -1.0)
        for ch in range(2):
            high, low = halves(acc[ch, :SLOTS, :])
            rhs[:, ch * LANES : (ch + 1) * LANES] = high
            rhs[:, (ch + 2) * LANES : (ch + 3) * LANES] = low
        upper, lower = within // 64, within % 64
        place = r.astype(F32)
        which = iota((8, LANES), 0)
        codes = []
        for g in range(groups):
            codes.append(
                jnp.where(
                    which == 0,
                    upper[g : g + 1, :],
                    jnp.where(which == 1, lower[g : g + 1, :], jnp.where(which == 2, 1, 0)),
                )
            )
        code = jnp.concatenate(codes, 1).astype(F32).astype(BF16)
        for v in range(N_VOL):
            chosen = jnp.concatenate(
                [
                    (place == key[v * groups + g : v * groups + g + 1, :]).astype(F32).astype(BF16)
                    for g in range(groups)
                ],
                1,
            )
            out = dot(chosen, rhs[...])
            send_ref[v, :CAP, :] = out[:, :LANES] + out[:, 2 * LANES : 3 * LANES]
            send_ref[v, FIRST:, :] = out[:, LANES : 2 * LANES] + out[:, 3 * LANES :]
            ids = lax.dot_general(code, chosen, (((1,), (1,)), ((), ())), preferred_element_type=F32)
            tile = ids[0:1] * 64.0 + ids[1:2] + ids[2:3] - 1.0
            send_ref[v, CAP:FIRST, :] = jnp.broadcast_to(tile, (8, LANES))


def project(kernel, pressure, velocity, entry_slot, slot_tile):
    rows = STEP // LANES
    return pl.pallas_call(
        project_kernel,
        grid=(ENTRIES // STEP,),
        out_shape=jax.ShapeDtypeStruct((N_VOL, MSG, LANES), F32),
        in_specs=[
            pl.BlockSpec((rows, LANES), lambda g: (g, 0), memory_space=pltpu.SMEM),
            pl.BlockSpec((STEP, LANES), lambda g: (g, 0)),
            pl.BlockSpec((rows, LANES), lambda g: (g, 0)),
            pl.BlockSpec((rows, LANES), lambda g: (g, 0)),
            pl.BlockSpec((rows, LANES), lambda g: (g, 0)),
            pl.BlockSpec((SLOTS // LANES, LANES), lambda g: (0, 0)),
        ],
        out_specs=pl.BlockSpec((N_VOL, MSG, LANES), lambda g: (0, 0, 0)),
        scratch_shapes=[
            pltpu.VMEM((2, SLOTS + WINDOW + 8, LANES), F32),
            pltpu.VMEM((SLOTS, 4 * LANES), BF16),
        ],
        compiler_params=pltpu.CompilerParams(dimension_semantics=("arbitrary",)),
        name="project",
    )(entry_slot, kernel, pressure, velocity, entry_slot, slot_tile)


GROUP = 4
HALF = BLOCK_TILES // 2
PIECE = HALF // SIDE
TALL = 256


def exchange_kernel(
    send, out, recv, acc, other, parts, rhs,
    p1s, p1r, d2s, d2r, rss, rsr, ags, agr, fws, fwr,
):
    vol = lax.axis_index("vol")
    pix = lax.axis_index("pix")
    x, core = pix // 2, pix % 2
    y, z = vol // SIDE, vol % SIDE

    def vol_to(k):
        return {"vol": lax.rem(y + k // SIDE, SIDE) * SIDE + lax.rem(z + k % SIDE, SIDE)}

    def pix_to(k):
        return {"pix": lax.rem(x + k, SIDE) * 2 + core}

    partner = {"pix": x * 2 + 1 - core}
    peers = [vol_to(k) for k in range(1, N_VOL)] + [pix_to(k) for k in range(1, SIDE)] + [partner]
    barrier = pltpu.get_barrier_semaphore()
    for peer in peers:
        pl.semaphore_signal(barrier, inc=1, device_id=peer, device_id_type=MESH)
    pl.semaphore_wait(barrier, len(peers))

    started = []

    def copy(src, dst, s, r, peer):
        c = pltpu.make_async_remote_copy(
            src_ref=src, dst_ref=dst, send_sem=s, recv_sem=r, device_id=peer, device_id_type=MESH
        )
        c.start()
        started.append(c)
        return c

    spans = ((0, FIRST), (FIRST, CAP))
    rows_of = (0, FIRST)
    first = [[None] * N_VOL for _ in range(2)]
    for ch in range(2):
        begin, size = spans[ch]
        for k in range(1, N_VOL):
            peer = vol_to(k)
            first[ch][k] = copy(
                send.at[peer["vol"], pl.ds(begin, size)],
                recv.at[k, pl.ds(begin, size)],
                p1s.at[ch, k], p1r.at[ch, k], peer,
            )

    def combine(ch, group):
        ids = []
        for n in range(GROUP):
            k = group * GROUP + n
            if k:
                first[ch][k].wait_recv()
                ids.append(recv[k, CAP : CAP + 1, :])
                rows = recv[k, rows_of[ch] : rows_of[ch] + CAP, :]
            else:
                ids.append(send[vol, CAP : CAP + 1, :])
                rows = send[vol, rows_of[ch] : rows_of[ch] + CAP, :]
            high, low = halves(rows)
            rhs[n * CAP : (n + 1) * CAP, :LANES] = high
            rhs[n * CAP : (n + 1) * CAP, LANES:] = low

        @pl.loop(0, BLOCK_TILES // TALL)
        def _(t):
            at = pl.multiple_of(t * TALL, TALL)
            tile = (iota((TALL, LANES), 0) + at).astype(F32)
            chosen = jnp.concatenate([(tile == i).astype(F32).astype(BF16) for i in ids], 1)
            both = dot(chosen, rhs[...])
            total = both[:, :LANES] + both[:, LANES:]
            if group:
                total += acc[ch, pl.ds(at, TALL), :]
            acc[ch, pl.ds(at, TALL), :] = total

    mine = core * HALF
    theirs = HALF - mine

    def swap(ch):
        return copy(acc.at[ch, pl.ds(theirs, HALF)], other.at[ch], d2s.at[ch], d2r.at[ch], partner)

    def reduce_start(ch, swapped):
        swapped.wait_recv()
        acc[ch, pl.ds(mine, HALF), :] += other[ch]
        copies = []
        for k in range(1, SIDE):
            at = pl.multiple_of(mine + lax.rem(x + k, SIDE) * PIECE, PIECE)
            copies.append(
                copy(acc.at[ch, pl.ds(at, PIECE)], parts.at[ch, k - 1], rss.at[ch, k - 1], rsr.at[ch, k - 1], pix_to(k))
            )
        return copies

    here = pl.multiple_of(mine + x * PIECE, PIECE)

    def gather_start(ch, copies):
        total = acc[ch, pl.ds(here, PIECE), :]
        for k in range(1, SIDE):
            copies[k - 1].wait_recv()
            total += parts[ch, k - 1]
        out[ch, pl.ds(here, PIECE), :] = total
        block = out.at[ch, pl.ds(here, PIECE)]
        gathers = [
            copy(block, block, ags.at[ch, k - 1], agr.at[ch, k - 1], pix_to(k)) for k in range(1, SIDE)
        ]
        return gathers, [copy(block, block, fws.at[ch, 0], fwr.at[ch, 0], partner)]

    def forward(ch, gathers, sent):
        for k in range(1, SIDE):
            gathers[k - 1].wait_recv()
            at = pl.multiple_of(mine + lax.rem(x - k + SIDE, SIDE) * PIECE, PIECE)
            block = out.at[ch, pl.ds(at, PIECE)]
            sent.append(copy(block, block, fws.at[ch, k], fwr.at[ch, k], partner))
        return sent

    groups = N_VOL // GROUP
    for g in range(groups):
        combine(0, g)
    s0 = swap(0)
    combine(1, 0)
    r0 = reduce_start(0, s0)
    combine(1, 1)
    a0, f0 = gather_start(0, r0)
    combine(1, 2)
    f0 = forward(0, a0, f0)
    combine(1, 3)
    s1 = swap(1)
    r1 = reduce_start(1, s1)
    a1, f1 = gather_start(1, r1)
    f1 = forward(1, a1, f1)
    for c in f0 + f1:
        c.wait_recv()
    for c in started:
        c.wait_send()


def exchange(send):
    vmem = pl.BlockSpec(memory_space=pltpu.VMEM)
    dma = pltpu.SemaphoreType.DMA
    return pl.pallas_call(
        exchange_kernel,
        out_shape=jax.ShapeDtypeStruct((2, BLOCK_TILES, LANES), F32),
        in_specs=[vmem],
        out_specs=vmem,
        scratch_shapes=[
            pltpu.VMEM((N_VOL, MSG, LANES), F32),
            pltpu.VMEM((2, BLOCK_TILES, LANES), F32),
            pltpu.VMEM((2, HALF, LANES), F32),
            pltpu.VMEM((2, SIDE - 1, PIECE, LANES), F32),
            pltpu.VMEM((GROUP * CAP, 2 * LANES), BF16),
            dma((2, N_VOL)), dma((2, N_VOL)),
            dma((2,)), dma((2,)),
            dma((2, SIDE - 1)), dma((2, SIDE - 1)),
            dma((2, SIDE - 1)), dma((2, SIDE - 1)),
            dma((2, SIDE)), dma((2, SIDE)),
        ],
        compiler_params=pltpu.CompilerParams(collective_id=0, has_side_effects=True),
        name="exchange",
    )(send)


def finish_kernel(map_ref, owner_ref, owned_ref, shell_ref, rhs):
    vol = lax.axis_index("vol")
    pix = lax.axis_index("pix")
    rows = BLOCK_TILES // LANES
    owner = owner_ref[pl.ds(pl.multiple_of(vol * rows, rows), rows), :]
    match = (owner == pix).astype(F32).astype(BF16)
    before = (iota((LANES, LANES), 0) < iota((LANES, LANES), 1)).astype(F32).astype(BF16)
    above = (iota((rows, rows), 1) < iota((rows, rows), 0)).astype(F32).astype(BF16)
    ones = jnp.ones((LANES, LANES), BF16)
    rank = dot(match, before) + dot(dot(above, match).astype(BF16), ones)
    key = jnp.where(match.astype(F32) > 0, rank, -1.0)
    for ch in range(2):
        value = map_ref[ch]
        shell_ref[:, ch * LANES : (ch + 1) * LANES] = value
        high, low = halves(value)
        rhs[:, ch * LANES : (ch + 1) * LANES] = high
        rhs[:, (ch + 2) * LANES : (ch + 3) * LANES] = low
    for t in range(OWN_MAX // TALL):
        place = (iota((TALL, LANES), 0) + t * TALL).astype(F32)
        chosen = jnp.concatenate(
            [(place == key[g : g + 1, :]).astype(F32).astype(BF16) for g in range(rows)], 1
        )
        both = dot(chosen, rhs[...])
        owned_ref[t * TALL : (t + 1) * TALL, :] = both[:, : 2 * LANES] + both[:, 2 * LANES :]


def finish(block_map, tile_owner):
    vmem = pl.BlockSpec(memory_space=pltpu.VMEM)
    return pl.pallas_call(
        finish_kernel,
        out_shape=(
            jax.ShapeDtypeStruct((OWN_MAX, 2 * LANES), F32),
            jax.ShapeDtypeStruct((BLOCK_TILES, 2 * LANES), F32),
        ),
        in_specs=[vmem, vmem],
        out_specs=(vmem, vmem),
        scratch_shapes=[pltpu.VMEM((BLOCK_TILES, 4 * LANES), BF16)],
        name="finish",
    )(block_map, tile_owner)


def shards(kernel, pressure, velocity, entry_slot, slot_tile, tile_owner):
    square = (ENTRIES // LANES, LANES)
    send = project(
        kernel,
        pressure.reshape(square),
        velocity.reshape(square),
        entry_slot.reshape(square),
        slot_tile.reshape(SLOTS // LANES, LANES),
    )
    block_map = exchange(send)
    return finish(block_map, tile_owner.reshape(-1, LANES))


def solution(mesh):
    in_specs = (
        P(("vol", "pix"), None),
        P(("vol", "pix")),
        P(("vol", "pix")),
        P(("vol", "pix"), None),
        P(("vol", "pix"), None),
        P(),
    )
    out_specs = (P(("vol", "pix"), None), P("vol", None))
    return jax.shard_map(shards, mesh=mesh, in_specs=in_specs, out_specs=out_specs, check_vma=False)
```

time: 451 us -> 92.8 us (0.21)
  other arithmetic: 228 us -> 0 us
  Pallas kernels: 0 us -> 90.3 us
  local copies, waits for them, and re-layouts: 82.9 us -> 0 us
  waiting for transfers between devices: 58.7 us -> 0 us
  matrix products: 43.1 us -> 0 us
  starting transfers between devices: 21.5 us -> 0 us
  between operations: 14.3 us -> 0.64 us
    scatter-add x17 -> x0, other arithmetic: 116 us -> none  [the longest x16 105 us: accumulate(): return (running.at[target_rows].add(pixel_products), None)]
    pallas_call x0 -> x3, Pallas kernels: none -> 90.3 us  [the longest x1 75.1 us: exchange(): pl.pallas_call(exchange_kernel, out_shape=jax.ShapeDtypeStruct((2, BLOCK_...]
    another operation x20 -> x0, other arithmetic: 78.1 us -> none
    reshape x34 -> x0, local copies, waits for them, and re-layouts: 44.2 us -> none  [the longest x16 24.6 us: accumulate(): pixel_products.reshape(group_size * block_rows, 2 * pixel_count)]
    dot_general x16 -> x0, matrix products: 43.1 us -> none  [accumulate(): jnp.einsum('vzc,vcx->vzx', particle_weights, kernel_weights, preferred_el...]
    all_to_all x2 -> x0, waiting for transfers between devices: 30.1 us -> none  [joined_exchange(): lax.all_to_all(blocks, axis, split_axis=0, concat_axis=0, tiled=True)]
    all_gather x1 -> x0, waiting for transfers between devices: 28.6 us -> none  [shards(): gathered_piece = lax.all_gather(owned, 'pix', axis=0, tiled=True)]
    select_n x35 -> x0, other arithmetic: 28.5 us -> none  [the longest x16 25.9 us: accumulate(): jnp.where(matches, thermal[:, None, :], nothing)]
  transfers between devices with their start and end apart: 3 -> 0, of which waited for: 2 -> 0; matrix products, arithmetic and copies ran while one was open for 60% -> 0% of each run, Pallas kernels for 0% -> 0%
where the time goes in v1:
time: 92.8 us; the launch traced here: 90.9 us
  Pallas kernels  90.3 us (97%)
    pallas_call x1, Pallas kernels, exchange(): pl.pallas_call(exchange_kernel, out_shape=jax.ShapeDtypeStruct((2, BLOCK_...  75.1 us
    pallas_call x1, Pallas kernels, project(): pl.pallas_call(project_kernel, grid=(ENTRIES // STEP,), out_shape=jax.Sha...  11.3 us
    pallas_call x1, Pallas kernels, finish(): pl.pallas_call(finish_kernel, out_shape=(jax.ShapeDtypeStruct((OWN_MAX, 2...  3.86 us

profile of v1, /device:TPU:1, one launch (start us, length us, event | category | flops | bytes accessed | tf_op | source)
XLA Modules:
  0.0 90.9 jit_solution(2584001919712729181)
XLA Ops:
  0.6 11.3 %project.1.send = f32[16,264,128]{2,1,0:T(8,128)} custom-call(s32[128,128]{1,0:T(8,128)} %bitcast.5, bf16[16384,128]{1,0:T(8,128)(2,1)} %kernel_ref.1, bf16[128,128]{1,0:T(8,128)(2,1)} %bitcast.8, bf16[128,128]{1,0:T(8,128)(2,1)} %bitcast.9, s32[128,128]{1,0:T(8,128)} %bitcast.6, s32[8,128]{1,0:T(8,128)} %bitcast.10), custom_call_target="tpu_custom_call" | custom-call | tf_op jit(solution)/shard_map/project/pallas_call | solution.py:132
  12.0 75.1 %exchange.1.map_ref = f32[2,2048,128]{2,1,0:T(8,128)} custom-call(f32[16,264,128]{2,1,0:T(8,128)} %project.1.send), custom_call_target="tpu_custom_call" | custom-call | tf_op jit(solution)/shard_map/exchange/pallas_call | solution.py:294
  87.1 3.9 %finish.1 = (f32[512,256]{1,0:T(8,128)}, f32[2048,256]{1,0:T(8,128)}) custom-call(f32[2,2048,128]{2,1,0:T(8,128)} %exchange.1.map_ref, s32[256,128]{1,0:T(8,128)} %bitcast.7), custom_call_target="tpu_custom_call" | custom-call | tf_op jit(solution)/shard_map/finish/pallas_call | solution.py:344

commit v2 on v1

v2 whole, which is shorter than its diff:
```python
import functools

import jax
import jax.numpy as jnp
from jax import lax
from jax.experimental import pallas as pl
from jax.experimental.pallas import tpu as pltpu
from jax.sharding import PartitionSpec as P

MESH = pl.DeviceIdType.MESH
F32 = jnp.float32
BF16 = jnp.bfloat16

LANES = 128
ENTRIES = 16384
SLOTS = 1024
N_VOL = 16
SIDE = 4
BLOCK_TILES = 2048
CAP = 128
OWN_MAX = 512

STEP = 2048
SPAN = 256
WINDOW = 32
MSG = 2 * CAP + 8
FIRST = CAP + 8


def dot(a, b):
    return jnp.dot(a, b, preferred_element_type=F32)


def iota(shape, dim):
    return lax.broadcasted_iota(jnp.int32, shape, dim)


def halves(x):
    high = x.astype(BF16)
    return high, (x - high.astype(F32)).astype(BF16)


def project_kernel(slot_s, kernel_ref, pressure_ref, velocity_ref, slot_ref, tile_ref, rhs_ref, key_ref, code_ref, acc):
    step = pl.program_id(0)

    @pl.when(step == 0)
    def _():
        acc[...] = jnp.zeros_like(acc)

    thermal = pressure_ref[...].astype(F32)
    kinetic = velocity_ref[...].astype(F32)
    slots = slot_ref[...]
    rows = iota((WINDOW, LANES), 0)

    def products(i, base):
        top, low = [], []
        for h in range(SPAN // LANES):
            r = i * (SPAN // LANES) + h
            match = rows == slots[r : r + 1, :] - base
            top.append(jnp.where(match, thermal[r : r + 1, :], 0.0))
            low.append(jnp.where(match, kinetic[r : r + 1, :], 0.0))
        weights = jnp.concatenate([jnp.concatenate(top, 1), jnp.concatenate(low, 1)], 0)
        return dot(weights.astype(BF16), kernel_ref[i * SPAN : (i + 1) * SPAN, :])

    def add(base, value):
        acc[0, pl.ds(base, WINDOW), :] += value[:WINDOW]
        acc[1, pl.ds(base, WINDOW), :] += value[WINDOW:]

    bases, lasts, values = [], [], []
    for i in range(STEP // SPAN):
        r = i * (SPAN // LANES)
        bases.append(pl.multiple_of((slot_s[r, 0] // 8) * 8, 8))
        lasts.append(slot_s[r + SPAN // LANES - 1, LANES - 1])
        values.append(products(i, bases[i]))
    for i in range(STEP // SPAN):
        add(bases[i], values[i])
    for i in range(STEP // SPAN):

        @pl.loop(1, (lasts[i] - bases[i]) // WINDOW + 1)
        def _(w, i=i):
            base = pl.multiple_of(bases[i] + w * WINDOW, 8)
            add(base, products(i, base))

    @pl.when(step == pl.num_programs(0) - 1)
    def _():
        tiles = tile_ref[...]
        block = tiles // BLOCK_TILES
        within = tiles - block * BLOCK_TILES
        groups = SLOTS // LANES
        match = jnp.concatenate([(block == v).astype(F32) for v in range(N_VOL)], 0).astype(BF16)
        r, c = iota((LANES, LANES), 0), iota((LANES, LANES), 1)
        before = (r < c).astype(F32).astype(BF16)
        above = ((c < r) & (c // groups == r // groups)).astype(F32).astype(BF16)
        ones = jnp.ones((LANES, LANES), BF16)
        rank = dot(match, before) + dot(dot(above, match).astype(BF16), ones)
        key_ref[...] = jnp.where(match.astype(F32) > 0, rank, -1.0)
        for ch in range(2):
            high, low = halves(acc[ch, :SLOTS, :])
            rhs_ref[:, ch * LANES : (ch + 1) * LANES] = high
            rhs_ref[:, (ch + 2) * LANES : (ch + 3) * LANES] = low
        upper, lower = within // 64, within % 64
        which = iota((8, LANES), 0)
        for g in range(groups):
            here = slice(g, g + 1)
            rest = jnp.where(which == 2, 1, 0)
            code = jnp.where(which == 0, upper[here], jnp.where(which == 1, lower[here], rest))
            code_ref[:, g * LANES : (g + 1) * LANES] = code.astype(F32).astype(BF16)


def project(kernel, pressure, velocity, entry_slot, slot_tile):
    rows = STEP // LANES
    outs = (((SLOTS, 4 * LANES), BF16), ((LANES, LANES), F32), ((8, SLOTS), BF16))
    return pl.pallas_call(
        project_kernel,
        grid=(ENTRIES // STEP,),
        out_shape=tuple(jax.ShapeDtypeStruct(*o) for o in outs),
        in_specs=[
            pl.BlockSpec((rows, LANES), lambda g: (g, 0), memory_space=pltpu.SMEM),
            pl.BlockSpec((STEP, LANES), lambda g: (g, 0)),
            pl.BlockSpec((rows, LANES), lambda g: (g, 0)),
            pl.BlockSpec((rows, LANES), lambda g: (g, 0)),
            pl.BlockSpec((rows, LANES), lambda g: (g, 0)),
            pl.BlockSpec((SLOTS // LANES, LANES), lambda g: (0, 0)),
        ],
        out_specs=tuple(pl.BlockSpec(o[0], lambda g: (0, 0)) for o in outs),
        scratch_shapes=[pltpu.VMEM((2, SLOTS + WINDOW + 8, LANES), F32)],
        compiler_params=pltpu.CompilerParams(dimension_semantics=("arbitrary",)),
        name="project",
    )(entry_slot, kernel, pressure, velocity, entry_slot, slot_tile)


GROUP = 4
SUBS = 2
HALF = BLOCK_TILES // 2
SUB = HALF // SUBS
PIECE = SUB // SIDE
TALL = 256
ORDER = tuple(range(N_VOL))


def equal(place, row):
    return jnp.where(place == row, jnp.ones((), BF16), jnp.zeros((), BF16))


def exchange_kernel(
    partial, keys, code, out, send, recv, acc, other, parts, rhs, hot,
    p1s, p1r, d2s, d2r, rss, rsr, ags, agr, fws, fwr,
):
    vol = lax.axis_index("vol")
    pix = lax.axis_index("pix")
    x, core = pix // 2, pix % 2
    y, z = vol // SIDE, vol % SIDE

    def vol_to(k):
        return lax.rem(y + k // SIDE, SIDE) * SIDE + lax.rem(z + k % SIDE, SIDE)

    def pix_to(k):
        return {"pix": lax.rem(x + k, SIDE) * 2 + core}

    partner = {"pix": x * 2 + 1 - core}
    peers = [{"vol": vol_to(k)} for k in range(1, N_VOL)] + [pix_to(k) for k in range(1, SIDE)] + [partner]
    barrier = pltpu.get_barrier_semaphore()
    for peer in peers:
        pl.semaphore_signal(barrier, inc=1, device_id=peer, device_id_type=MESH)

    started = []

    def copy(src, dst, s, r, peer):
        c = pltpu.make_async_remote_copy(
            src_ref=src, dst_ref=dst, send_sem=s, recv_sem=r, device_id=peer, device_id_type=MESH
        )
        c.start()
        started.append(c)
        return c

    spans = ((0, FIRST), (FIRST, CAP))
    rows_of = (0, FIRST)
    first = [[None] * N_VOL for _ in range(2)]

    def launch(ch, k):
        begin, size = spans[ch]
        to = vol_to(k)
        first[ch][k] = copy(
            send.at[k, pl.ds(begin, size)],
            recv.at[k, pl.ds(begin, size)],
            p1s.at[ch, k], p1r.at[ch, k], {"vol": to},
        )

    place = iota((CAP, LANES), 0).astype(F32).astype(BF16)

    def message(k):
        groups = SLOTS // LANES
        key = keys[pl.ds(pl.multiple_of(vol_to(k) * groups, groups), groups), :]
        chosen = jnp.concatenate(
            [equal(place, key[g : g + 1, :].astype(BF16)) for g in range(groups)], 1
        )
        both = dot(chosen, partial[...])
        send[k, :CAP, :] = both[:, :LANES] + both[:, 2 * LANES : 3 * LANES]
        send[k, FIRST:, :] = both[:, LANES : 2 * LANES] + both[:, 3 * LANES :]
        ids = lax.dot_general(code[...], chosen, (((1,), (1,)), ((), ())), preferred_element_type=F32)
        tile = ids[0:1] * 64.0 + ids[1:2] + ids[2:3] - 1.0
        send[k, CAP:FIRST, :] = jnp.broadcast_to(tile, (8, LANES))

    todo = ORDER[1:] + ORDER[:1]
    with jax.named_scope("messages"):
        for n, k in enumerate(todo):
            message(k)
            if n == 0:
                pl.semaphore_wait(barrier, len(peers))
            else:
                launch(0, todo[n - 1])
        for k in ORDER[1:]:
            launch(1, k)

    tall = iota((TALL, LANES), 0).astype(F32).astype(BF16)
    mine = core * HALF
    theirs = HALF - mine
    turn = GROUP * CAP

    def load(ch, group):
        ids = []
        for n in range(GROUP):
            k = ORDER[group * GROUP + n]
            source = recv if k else send
            if k:
                first[ch][k].wait_recv()
            ids.append(source[k, CAP : CAP + 1, :])
            high, low = halves(source[k, rows_of[ch] : rows_of[ch] + CAP, :])
            rhs[n * CAP : (n + 1) * CAP, :LANES] = high
            rhs[n * CAP : (n + 1) * CAP, LANES:] = low
        return ids

    def tiles(ch, group, ids, begin, size):
        columns = slice(group * turn, (group + 1) * turn)

        @pl.loop(0, size // TALL)
        def _(t):
            at = pl.multiple_of(begin + t * TALL, TALL)
            if ch == 0:
                pieces = []
                for i in ids:
                    local = i - at.astype(F32)
                    local = jnp.where((local >= 0) & (local < TALL), local, -1.0)
                    pieces.append(equal(tall, local.astype(BF16)))
                chosen = jnp.concatenate(pieces, 1)
                hot[pl.ds(at, TALL), columns] = chosen
            else:
                chosen = hot[pl.ds(at, TALL), columns]
            both = dot(chosen, rhs[...])
            total = both[:, :LANES] + both[:, LANES:]
            if group:
                total += acc[ch, pl.ds(at, TALL), :]
            acc[ch, pl.ds(at, TALL), :] = total

    def combine(ch, group):
        with jax.named_scope(f"load{ch}{group}"):
            ids = load(ch, group)
        with jax.named_scope(f"combine{ch}{group}"):
            tiles(ch, group, ids, 0, BLOCK_TILES)

    def combine_swap(ch, group):
        with jax.named_scope(f"load{ch}{group}"):
            ids = load(ch, group)
        copies = []
        with jax.named_scope(f"combine{ch}{group}"):
            for s in range(SUBS):
                tiles(ch, group, ids, theirs + s * SUB, SUB)
                at = pl.multiple_of(theirs + s * SUB, SUB)
                copies.append(
                    copy(acc.at[ch, pl.ds(at, SUB)], other.at[ch, s], d2s.at[ch, s], d2r.at[ch, s], partner)
                )
            tiles(ch, group, ids, mine, HALF)
        return copies

    def reduce_start(ch, s, swapped):
        with jax.named_scope(f"reduce{ch}{s}"):
            swapped.wait_recv()
            acc[ch, pl.ds(pl.multiple_of(mine + s * SUB, SUB), SUB), :] += other[ch, s]
            copies = []
            for k in (2, 1, 3):
                at = pl.multiple_of(mine + s * SUB + lax.rem(x + k, SIDE) * PIECE, PIECE)
                copies.append(
                    copy(
                        acc.at[ch, pl.ds(at, PIECE)], parts.at[ch, s, k - 1],
                        rss.at[ch, s, k - 1], rsr.at[ch, s, k - 1], pix_to(k),
                    )
                )
        return copies

    def gather_start(ch, s, copies):
        with jax.named_scope(f"gather{ch}{s}"):
            here = pl.multiple_of(mine + s * SUB + x * PIECE, PIECE)
            for c in copies:
                c.wait_recv()
            total = acc[ch, pl.ds(here, PIECE), :]
            for k in range(1, SIDE):
                total += parts[ch, s, k - 1]
            out[ch, pl.ds(here, PIECE), :] = total
            block = out.at[ch, pl.ds(here, PIECE)]
            gathers = [
                (k, copy(block, block, ags.at[ch, s, k - 1], agr.at[ch, s, k - 1], pix_to(k))) for k in (2, 1, 3)
            ]
        return gathers, [copy(block, block, fws.at[ch, s, 0], fwr.at[ch, s, 0], partner)]

    def forward(ch, s, started_gathers):
        gathers, sent = started_gathers
        with jax.named_scope(f"forward{ch}{s}"):
            for k, c in (gathers[1], gathers[2], gathers[0]):
                c.wait_recv()
                at = pl.multiple_of(mine + s * SUB + lax.rem(x - k + SIDE, SIDE) * PIECE, PIECE)
                block = out.at[ch, pl.ds(at, PIECE)]
                sent.append(copy(block, block, fws.at[ch, s, k], fwr.at[ch, s, k], partner))
        return sent

    for g in range(3):
        combine(0, g)
    s0 = combine_swap(0, 3)
    combine(1, 0)
    r0 = [reduce_start(0, s, s0[s]) for s in range(SUBS)]
    combine(1, 1)
    combine(1, 2)
    g0 = [gather_start(0, s, r0[s]) for s in range(SUBS)]
    s1 = combine_swap(1, 3)
    r1 = [reduce_start(1, s, s1[s]) for s in range(SUBS)]
    f0 = [forward(0, s, g0[s]) for s in range(SUBS)]
    g1 = [gather_start(1, s, r1[s]) for s in range(SUBS)]
    f1 = [forward(1, s, g1[s]) for s in range(SUBS)]
    with jax.named_scope("last"):
        for f in f0 + f1:
            for c in f:
                c.wait_recv()
        for c in started:
            c.wait_send()


def exchange(partial, keys, code):
    vmem = pl.BlockSpec(memory_space=pltpu.VMEM)
    dma = pltpu.SemaphoreType.DMA
    return pl.pallas_call(
        exchange_kernel,
        out_shape=jax.ShapeDtypeStruct((2, BLOCK_TILES, LANES), F32),
        in_specs=[vmem] * 3,
        out_specs=vmem,
        scratch_shapes=[
            pltpu.VMEM((N_VOL, MSG, LANES), F32),
            pltpu.VMEM((N_VOL, MSG, LANES), F32),
            pltpu.VMEM((2, BLOCK_TILES, LANES), F32),
            pltpu.VMEM((2, SUBS, SUB, LANES), F32),
            pltpu.VMEM((2, SUBS, SIDE - 1, PIECE, LANES), F32),
            pltpu.VMEM((GROUP * CAP, 2 * LANES), BF16),
            pltpu.VMEM((BLOCK_TILES, N_VOL * CAP), BF16),
            dma((2, N_VOL)), dma((2, N_VOL)),
            dma((2, SUBS)), dma((2, SUBS)),
            dma((2, SUBS, SIDE - 1)), dma((2, SUBS, SIDE - 1)),
            dma((2, SUBS, SIDE - 1)), dma((2, SUBS, SIDE - 1)),
            dma((2, SUBS, SIDE)), dma((2, SUBS, SIDE)),
        ],
        compiler_params=pltpu.CompilerParams(collective_id=0, has_side_effects=True),
        name="exchange",
    )(partial, keys, code)


def finish_kernel(map_ref, owner_ref, owned_ref, shell_ref, rhs):
    vol = lax.axis_index("vol")
    pix = lax.axis_index("pix")
    rows = BLOCK_TILES // LANES
    owner = owner_ref[pl.ds(pl.multiple_of(vol * rows, rows), rows), :]
    match = (owner == pix).astype(F32).astype(BF16)
    before = (iota((LANES, LANES), 0) < iota((LANES, LANES), 1)).astype(F32).astype(BF16)
    above = (iota((rows, rows), 1) < iota((rows, rows), 0)).astype(F32).astype(BF16)
    ones = jnp.ones((LANES, LANES), BF16)
    rank = dot(match, before) + dot(dot(above, match).astype(BF16), ones)
    key = jnp.where(match.astype(F32) > 0, rank, -1.0)
    for ch in range(2):
        value = map_ref[ch]
        shell_ref[:, ch * LANES : (ch + 1) * LANES] = value
        high, low = halves(value)
        rhs[:, ch * LANES : (ch + 1) * LANES] = high
        rhs[:, (ch + 2) * LANES : (ch + 3) * LANES] = low
    for t in range(OWN_MAX // TALL):
        place = (iota((TALL, LANES), 0) + t * TALL).astype(F32)
        chosen = jnp.concatenate(
            [(place == key[g : g + 1, :]).astype(F32).astype(BF16) for g in range(rows)], 1
        )
        both = dot(chosen, rhs[...])
        owned_ref[t * TALL : (t + 1) * TALL, :] = both[:, : 2 * LANES] + both[:, 2 * LANES :]


def finish(block_map, tile_owner):
    vmem = pl.BlockSpec(memory_space=pltpu.VMEM)
    return pl.pallas_call(
        finish_kernel,
        out_shape=(
            jax.ShapeDtypeStruct((OWN_MAX, 2 * LANES), F32),
            jax.ShapeDtypeStruct((BLOCK_TILES, 2 * LANES), F32),
        ),
        in_specs=[vmem, vmem],
        out_specs=(vmem, vmem),
        scratch_shapes=[pltpu.VMEM((BLOCK_TILES, 4 * LANES), BF16)],
        name="finish",
    )(block_map, tile_owner)


def shards(kernel, pressure, velocity, entry_slot, slot_tile, tile_owner):
    square = (ENTRIES // LANES, LANES)
    partial, keys, code = project(
        kernel,
        pressure.reshape(square),
        velocity.reshape(square),
        entry_slot.reshape(square),
        slot_tile.reshape(SLOTS // LANES, LANES),
    )
    block_map = exchange(partial, keys, code)
    return finish(block_map, tile_owner.reshape(-1, LANES))


def solution(mesh):
    in_specs = (
        P(("vol", "pix"), None),
        P(("vol", "pix")),
        P(("vol", "pix")),
        P(("vol", "pix"), None),
        P(("vol", "pix"), None),
        P(),
    )
    out_specs = (P(("vol", "pix"), None), P("vol", None))
    return jax.shard_map(shards, mesh=mesh, in_specs=in_specs, out_specs=out_specs, check_vma=False)
```

time: 92.8 us -> 74.8 us (0.81); the launches traced: 90.9 us -> 74.5 us
  Pallas kernels: 90.3 us -> 73.9 us
    pallas_call x1, Pallas kernels: 75.1 us -> 62.4 us  [exchange(): pl.pallas_call(exchange_kernel, out_shape=jax.ShapeDtypeStruct((2, BLOCK_...]
    pallas_call x1, Pallas kernels: 11.3 us -> 7.69 us  [project(): pl.pallas_call(project_kernel, grid=(ENTRIES // STEP,), out_shape=tuple((...]
where the time goes in v2:
time: 74.8 us; the launch traced here: 74.5 us
  Pallas kernels  73.9 us (99%)
    pallas_call x1, Pallas kernels, exchange(): pl.pallas_call(exchange_kernel, out_shape=jax.ShapeDtypeStruct((2, BLOCK_...  62.4 us
    pallas_call x1, Pallas kernels, project(): pl.pallas_call(project_kernel, grid=(ENTRIES // STEP,), out_shape=tuple((...  7.69 us
    pallas_call x1, Pallas kernels, finish(): pl.pallas_call(finish_kernel, out_shape=(jax.ShapeDtypeStruct((OWN_MAX, 2...  3.86 us

profile of v2, /device:TPU:1, one launch (start us, length us, event | category | flops | bytes accessed | tf_op | source)
XLA Modules:
  0.0 74.5 jit_solution(12599568427603284997)
XLA Ops:
  0.6 7.7 %project.1 = (bf16[1024,512]{1,0:T(8,128)(2,1)}, f32[128,128]{1,0:T(8,128)}, bf16[8,1024]{1,0:T(8,128)(2,1)}) custom-call(s32[128,128]{1,0:T(8,128)} %bitcast.5, bf16[16384,128]{1,0:T(8,128)(2,1)} %kernel_ref.1, bf16[128,128]{1,0:T(8,128)(2,1)} %bitcast.8, bf16[128,128]{1,0:T(8,128)(2,1)} %bitcast.9, s32[128,128]{1,0:T(8,128)} %bitcast.6, s32[8,128]{1,0:T(8,128)} %bitcast.10), custom_call_target="tpu_custom_call" | custom-call | tf_op jit(solution)/shard_map/project/pallas_call | solution.py:113
  8.3 62.4 %exchange.1.map_ref = f32[2,2048,128]{2,1,0:T(8,128)} custom-call(bf16[1024,512]{1,0:T(8,128)(2,1)} %get-tuple-element.5.partial, f32[128,128]{1,0:T(8,128)} %get-tuple-element.6.keys, bf16[8,1024]{1,0:T(8,128)(2,1)} %get-tuple-element.7.code), custom_call_target="tpu_custom_call" | custom-call | tf_op jit(solution)/shard_map/exchange/pallas_call | solution.py:339
  70.7 3.9 %finish.1 = (f32[512,256]{1,0:T(8,128)}, f32[2048,256]{1,0:T(8,128)}) custom-call(f32[2,2048,128]{2,1,0:T(8,128)} %exchange.1.map_ref, s32[256,128]{1,0:T(8,128)} %bitcast.7), custom_call_target="tpu_custom_call" | custom-call | tf_op jit(solution)/shard_map/finish/pallas_call | solution.py:391

commit v3 on v2

v3 whole, which is shorter than its diff:
```python
import functools

import jax
import jax.numpy as jnp
from jax import lax
from jax.experimental import pallas as pl
from jax.experimental.pallas import tpu as pltpu
from jax.sharding import PartitionSpec as P

MESH = pl.DeviceIdType.MESH
F32 = jnp.float32
BF16 = jnp.bfloat16

LANES = 128
ENTRIES = 16384
SLOTS = 1024
N_VOL = 16
SIDE = 4
BLOCK_TILES = 2048
CAP = 128
OWN_MAX = 512

STEP = 2048
SPAN = 256
WINDOW = 32
MSG = 2 * CAP + 8
FIRST = CAP + 8


def dot(a, b):
    return jnp.dot(a, b, preferred_element_type=F32)


def iota(shape, dim):
    return lax.broadcasted_iota(jnp.int32, shape, dim)


def halves(x):
    high = x.astype(BF16)
    return high, (x - high.astype(F32)).astype(BF16)


def equal(place, row):
    return jnp.where(place == row, jnp.ones((), BF16), jnp.zeros((), BF16))


def project_kernel(
    kernel_h, pressure_h, velocity_h, slot_h, tile_h, rhs_ref, key_ref, ids_ref,
    weights, pressure, velocity, slot_v, tile_v, slot_s, acc, sems, chunk_sems,
):
    steps = ENTRIES // STEP
    rows = STEP // LANES
    small = [
        pltpu.make_async_copy(a, b, sems.at[n])
        for n, (a, b) in enumerate(
            (
                (tile_h, tile_v), (slot_h, slot_s), (slot_h, slot_v),
                (pressure_h, pressure), (velocity_h, velocity),
            )
        )
    ]
    for c in small:
        c.start()

    def chunk(g):
        span = pl.ds(pl.multiple_of(g * STEP, STEP), STEP)
        return pltpu.make_async_copy(kernel_h.at[span], weights.at[span], chunk_sems.at[g])

    for g in range(steps):
        chunk(g).start()
    acc[...] = jnp.zeros_like(acc)

    small[0].wait()
    tiles = tile_v[...]
    block = tiles // BLOCK_TILES
    within = tiles - block * BLOCK_TILES
    groups = SLOTS // LANES
    match = jnp.concatenate([(block == v).astype(F32) for v in range(N_VOL)], 0)
    r, c = iota((LANES, LANES), 0), iota((LANES, LANES), 1)
    before = (r < c).astype(F32).astype(BF16)
    above = ((c < r) & (c // groups == r // groups)).astype(F32).astype(BF16)
    ones = jnp.ones((LANES, LANES), BF16)
    packed = match.astype(BF16)
    rank = dot(packed, before) + dot(dot(above, packed).astype(BF16), ones)
    key_ref[...] = jnp.where(match > 0, rank, -1.0)
    own = jnp.zeros((groups, LANES), F32)
    for v in range(N_VOL):
        own += match[v * groups : (v + 1) * groups] * rank[v * groups : (v + 1) * groups]
    place = iota((LANES, LANES), 0).astype(F32).astype(BF16)
    spread = jnp.concatenate([equal(place, own[g : g + 1].astype(BF16)) for g in range(groups)], 1)
    vols = iota((N_VOL, LANES), 0)
    upper, lower = (within // 64).astype(F32), (within % 64).astype(F32)
    table = []
    for values in (upper, lower, jnp.ones_like(upper)):
        table.append(
            jnp.concatenate(
                [jnp.where(vols == block[g : g + 1], values[g : g + 1], 0.0) for g in range(groups)], 1
            )
        )
    table = jnp.concatenate(table, 0).astype(BF16)
    found = lax.dot_general(table, spread, (((1,), (1,)), ((), ())), preferred_element_type=F32)
    ids_ref[...] = found[:N_VOL] * 64.0 + found[N_VOL : 2 * N_VOL] + found[2 * N_VOL :] - 1.0

    for n in (1, 2, 3, 4):
        small[n].wait()
    lines = iota((WINDOW, LANES), 0)
    per = SPAN // LANES

    @pl.loop(0, steps)
    def _(g):
        chunk(g).wait()
        top = pl.multiple_of(g * rows, rows)
        thermal = pressure[pl.ds(top, rows), :].astype(F32)
        kinetic = velocity[pl.ds(top, rows), :].astype(F32)
        slots = slot_v[pl.ds(top, rows), :]

        def products(i, base):
            up, low = [], []
            for h in range(per):
                n = i * per + h
                match = lines == slots[n : n + 1, :] - base
                up.append(jnp.where(match, thermal[n : n + 1, :], 0.0))
                low.append(jnp.where(match, kinetic[n : n + 1, :], 0.0))
            amplitudes = jnp.concatenate([jnp.concatenate(up, 1), jnp.concatenate(low, 1)], 0)
            span = pl.ds(pl.multiple_of(g * STEP + i * SPAN, SPAN), SPAN)
            return dot(amplitudes.astype(BF16), weights[span, :])

        def add(base, value):
            acc[0, pl.ds(base, WINDOW), :] += value[:WINDOW]
            acc[1, pl.ds(base, WINDOW), :] += value[WINDOW:]

        count = STEP // SPAN
        bases, lasts = [], []
        for i in range(count):
            bases.append(pl.multiple_of((slot_s[top + i * per, 0] // 8) * 8, 8))
            lasts.append(slot_s[top + i * per + per - 1, LANES - 1])
        values = [products(i, bases[i]) for i in range(count)]
        for i in range(count):
            add(bases[i], values[i])
        for i in range(count):

            @pl.loop(1, (lasts[i] - bases[i]) // WINDOW + 1)
            def _(w, i=i):
                base = pl.multiple_of(bases[i] + w * WINDOW, 8)
                add(base, products(i, base))

    for ch in range(2):
        high, low = halves(acc[ch, :SLOTS, :])
        rhs_ref[:, 2 * ch * LANES : (2 * ch + 1) * LANES] = high
        rhs_ref[:, (2 * ch + 1) * LANES : (2 * ch + 2) * LANES] = low


def project(kernel, pressure, velocity, entry_slot, slot_tile):
    outs = (((SLOTS, 4 * LANES), BF16), ((LANES, LANES), F32), ((N_VOL, LANES), F32))
    square = (ENTRIES // LANES, LANES)
    return pl.pallas_call(
        project_kernel,
        out_shape=tuple(jax.ShapeDtypeStruct(*o) for o in outs),
        in_specs=[pl.BlockSpec(memory_space=pltpu.HBM)] * 5,
        out_specs=tuple(pl.BlockSpec(memory_space=pltpu.VMEM) for o in outs),
        scratch_shapes=[
            pltpu.VMEM((ENTRIES, LANES), BF16),
            pltpu.VMEM(square, BF16),
            pltpu.VMEM(square, BF16),
            pltpu.VMEM(square, jnp.int32),
            pltpu.VMEM((SLOTS // LANES, LANES), jnp.int32),
            pltpu.SMEM(square, jnp.int32),
            pltpu.VMEM((2, SLOTS + WINDOW + 8, LANES), F32),
            pltpu.SemaphoreType.DMA((5,)),
            pltpu.SemaphoreType.DMA((ENTRIES // STEP,)),
        ],
        compiler_params=pltpu.CompilerParams(vmem_limit_bytes=16 << 20),
        name="project",
    )(*(pltpu.with_memory_space_constraint(a, pltpu.HBM) for a in (kernel, pressure, velocity, entry_slot, slot_tile)))


GROUP = 4
SUBS = 2
HALF = BLOCK_TILES // 2
SUB = HALF // SUBS
PIECE = SUB // SIDE
TALL = 1024
BAND = 256
ORDER = (0, 1, 4, 3, 12, 5, 15, 7, 13, 2, 8, 6, 9, 10, 14, 11)
ROUND = 4


def exchange_kernel(
    partial, keys, ids_ref, out, send, recv, acc, other, parts, rhs, hot, pick,
    p1s, p1r, d2s, d2r, rss, rsr, ags, agr, fws, fwr,
):
    vol = lax.axis_index("vol")
    pix = lax.axis_index("pix")
    x, core = pix // 2, pix % 2
    y, z = vol // SIDE, vol % SIDE

    def vol_to(k):
        return lax.rem(y + k // SIDE, SIDE) * SIDE + lax.rem(z + k % SIDE, SIDE)

    def pix_to(k):
        return {"pix": lax.rem(x + k, SIDE) * 2 + core}

    partner = {"pix": x * 2 + 1 - core}
    peers = [{"vol": vol_to(k)} for k in range(1, N_VOL)] + [pix_to(k) for k in range(1, SIDE)] + [partner]
    barrier = pltpu.get_barrier_semaphore()
    for peer in peers:
        pl.semaphore_signal(barrier, inc=1, device_id=peer, device_id_type=MESH)

    started = []

    def copy(src, dst, s, r, peer):
        c = pltpu.make_async_remote_copy(
            src_ref=src, dst_ref=dst, send_sem=s, recv_sem=r, device_id=peer, device_id_type=MESH
        )
        c.start()
        started.append(c)
        return c

    spans = ((0, FIRST), (FIRST, CAP))
    rows_of = (0, FIRST)
    first = [[None] * N_VOL for _ in range(2)]

    def launch(ch, k):
        begin, size = spans[ch]
        to = vol_to(k)
        first[ch][k] = copy(
            send.at[k, pl.ds(begin, size)],
            recv.at[k, pl.ds(begin, size)],
            p1s.at[ch, k], p1r.at[ch, k], {"vol": to},
        )

    place = iota((CAP, LANES), 0).astype(F32).astype(BF16)
    groups = SLOTS // LANES

    def batch(ch, n, ks):
        here = slice(n * CAP, (n + len(ks)) * CAP)
        if ch == 0:
            for m, k in enumerate(ks):
                key = keys[pl.ds(pl.multiple_of(vol_to(k) * groups, groups), groups), :]
                pick[(n + m) * CAP : (n + m + 1) * CAP, :] = jnp.concatenate(
                    [equal(place, key[g : g + 1, :].astype(BF16)) for g in range(groups)], 1
                )
                send[k, CAP:FIRST, :] = jnp.broadcast_to(ids_ref[pl.ds(vol_to(k), 1), :], (8, LANES))
        both = dot(pick[here, :], partial[:, 2 * ch * LANES : 2 * (ch + 1) * LANES])
        total = both[:, :LANES] + both[:, LANES:]
        for m, k in enumerate(ks):
            send[k, rows_of[ch] : rows_of[ch] + CAP, :] = total[m * CAP : (m + 1) * CAP]

    todo = ORDER[1:] + ORDER[:1]
    waiting = []
    with jax.named_scope("messages"):
        for ch in range(2):
            for n in range(0, N_VOL, ROUND):
                ks = todo[n : n + ROUND]
                batch(ch, n, ks)
                if ch == 0 and n == 0:
                    pl.semaphore_wait(barrier, len(peers))
                for c, k in waiting:
                    launch(c, k)
                waiting = [(ch, k) for k in ks if k]
        for c, k in waiting:
            launch(c, k)

    band = iota((BAND, LANES), 0).astype(F32).astype(BF16)
    mine = core * HALF
    theirs = HALF - mine
    turn = GROUP * CAP

    def load(ch, group):
        ids = []
        for n in range(GROUP):
            k = ORDER[group * GROUP + n]
            source = recv if k else send
            if k:
                first[ch][k].wait_recv()
            ids.append(source[k, CAP : CAP + 1, :])
            high, low = halves(source[k, rows_of[ch] : rows_of[ch] + CAP, :])
            rhs[n * CAP : (n + 1) * CAP, :LANES] = high
            rhs[n * CAP : (n + 1) * CAP, LANES:] = low
        return ids

    def tiles(ch, group, ids, begin, count):
        columns = slice(group * turn, (group + 1) * turn)

        def one(t):
            at = pl.multiple_of(begin + t * TALL, TALL)
            if ch == 0:
                for b in range(TALL // BAND):
                    low = pl.multiple_of(at + b * BAND, BAND)
                    pieces = []
                    for i in ids:
                        local = i - low.astype(F32)
                        local = jnp.where((local >= 0) & (local < BAND), local, -1.0)
                        pieces.append(equal(band, local.astype(BF16)))
                    hot[pl.ds(low, BAND), columns] = jnp.concatenate(pieces, 1)
            both = dot(hot[pl.ds(at, TALL), columns], rhs[...])
            total = both[:, :LANES] + both[:, LANES:]
            if group:
                total += acc[ch, pl.ds(at, TALL), :]
            acc[ch, pl.ds(at, TALL), :] = total

        if count == 1:
            one(0)
        else:
            pl.loop(0, count)(one)

    def combine(ch, group):
        with jax.named_scope(f"load{ch}{group}"):
            ids = load(ch, group)
        with jax.named_scope(f"combine{ch}{group}"):
            tiles(ch, group, ids, jnp.int32(0), BLOCK_TILES // TALL)

    def combine_swap(ch, group):
        with jax.named_scope(f"load{ch}{group}"):
            ids = load(ch, group)
        copies = []
        with jax.named_scope(f"combine{ch}{group}"):
            tiles(ch, group, ids, theirs, HALF // TALL)
            for s in range(SUBS):
                at = pl.multiple_of(theirs + s * SUB, SUB)
                copies.append(
                    copy(acc.at[ch, pl.ds(at, SUB)], other.at[ch, s], d2s.at[ch, s], d2r.at[ch, s], partner)
                )
            tiles(ch, group, ids, mine, HALF // TALL)
        return copies

    def reduce_start(ch, s, swapped):
        with jax.named_scope(f"reduce{ch}{s}"):
            swapped.wait_recv()
            acc[ch, pl.ds(pl.multiple_of(mine + s * SUB, SUB), SUB), :] += other[ch, s]
            copies = []
            for k in (2, 1, 3):
                at = pl.multiple_of(mine + s * SUB + lax.rem(x + k, SIDE) * PIECE, PIECE)
                copies.append(
                    copy(
                        acc.at[ch, pl.ds(at, PIECE)], parts.at[ch, s, k - 1],
                        rss.at[ch, s, k - 1], rsr.at[ch, s, k - 1], pix_to(k),
                    )
                )
        return copies

    def gather_start(ch, s, copies):
        with jax.named_scope(f"gather{ch}{s}"):
            here = pl.multiple_of(mine + s * SUB + x * PIECE, PIECE)
            for c in copies:
                c.wait_recv()
            total = acc[ch, pl.ds(here, PIECE), :]
            for k in range(1, SIDE):
                total += parts[ch, s, k - 1]
            out[ch, pl.ds(here, PIECE), :] = total
            block = out.at[ch, pl.ds(here, PIECE)]
            gathers = [
                (k, copy(block, block, ags.at[ch, s, k - 1], agr.at[ch, s, k - 1], pix_to(k))) for k in (2, 1, 3)
            ]
        return gathers, [copy(block, block, fws.at[ch, s, 0], fwr.at[ch, s, 0], partner)]

    def forward(ch, s, started_gathers):
        gathers, sent = started_gathers
        with jax.named_scope(f"forward{ch}{s}"):
            for k, c in (gathers[1], gathers[2], gathers[0]):
                c.wait_recv()
                at = pl.multiple_of(mine + s * SUB + lax.rem(x - k + SIDE, SIDE) * PIECE, PIECE)
                block = out.at[ch, pl.ds(at, PIECE)]
                sent.append(copy(block, block, fws.at[ch, s, k], fwr.at[ch, s, k], partner))
        return sent

    for g in range(3):
        combine(0, g)
    s0 = combine_swap(0, 3)
    combine(1, 0)
    r0 = [reduce_start(0, s, s0[s]) for s in range(SUBS)]
    combine(1, 1)
    combine(1, 2)
    g0 = [gather_start(0, s, r0[s]) for s in range(SUBS)]
    s1 = combine_swap(1, 3)
    r1 = [reduce_start(1, s, s1[s]) for s in range(SUBS)]
    f0 = [forward(0, s, g0[s]) for s in range(SUBS)]
    g1 = [gather_start(1, s, r1[s]) for s in range(SUBS)]
    f1 = [forward(1, s, g1[s]) for s in range(SUBS)]
    with jax.named_scope("last"):
        for f in f0 + f1:
            for c in f:
                c.wait_recv()
        for c in started:
            c.wait_send()


def exchange(partial, keys, ids):
    vmem = pl.BlockSpec(memory_space=pltpu.VMEM)
    dma = pltpu.SemaphoreType.DMA
    return pl.pallas_call(
        exchange_kernel,
        out_shape=jax.ShapeDtypeStruct((2, BLOCK_TILES, LANES), F32),
        in_specs=[vmem] * 3,
        out_specs=vmem,
        scratch_shapes=[
            pltpu.VMEM((N_VOL, MSG, LANES), F32),
            pltpu.VMEM((N_VOL, MSG, LANES), F32),
            pltpu.VMEM((2, BLOCK_TILES, LANES), F32),
            pltpu.VMEM((2, SUBS, SUB, LANES), F32),
            pltpu.VMEM((2, SUBS, SIDE - 1, PIECE, LANES), F32),
            pltpu.VMEM((GROUP * CAP, 2 * LANES), BF16),
            pltpu.VMEM((BLOCK_TILES, N_VOL * CAP), BF16),
            pltpu.VMEM((N_VOL * CAP, SLOTS), BF16),
            dma((2, N_VOL)), dma((2, N_VOL)),
            dma((2, SUBS)), dma((2, SUBS)),
            dma((2, SUBS, SIDE - 1)), dma((2, SUBS, SIDE - 1)),
            dma((2, SUBS, SIDE - 1)), dma((2, SUBS, SIDE - 1)),
            dma((2, SUBS, SIDE)), dma((2, SUBS, SIDE)),
        ],
        compiler_params=pltpu.CompilerParams(
            collective_id=0, has_side_effects=True, vmem_limit_bytes=32 << 20
        ),
        name="exchange",
    )(partial, keys, ids)


def finish_kernel(map_ref, owner_ref, owned_ref, shell_h, rhs, sems):
    vol = lax.axis_index("vol")
    pix = lax.axis_index("pix")
    copies = []
    for ch in range(2):
        c = pltpu.make_async_copy(
            map_ref.at[ch], shell_h.at[:, pl.ds(ch * LANES, LANES)], sems.at[ch]
        )
        c.start()
        copies.append(c)
    rows = BLOCK_TILES // LANES
    owner = owner_ref[pl.ds(pl.multiple_of(vol * rows, rows), rows), :]
    match = (owner == pix).astype(F32).astype(BF16)
    before = (iota((LANES, LANES), 0) < iota((LANES, LANES), 1)).astype(F32).astype(BF16)
    above = (iota((rows, rows), 1) < iota((rows, rows), 0)).astype(F32).astype(BF16)
    ones = jnp.ones((LANES, LANES), BF16)
    rank = dot(match, before) + dot(dot(above, match).astype(BF16), ones)
    key = jnp.where(match.astype(F32) > 0, rank, -1.0)
    for ch in range(2):
        high, low = halves(map_ref[ch])
        rhs[:, ch * LANES : (ch + 1) * LANES] = high
        rhs[:, (ch + 2) * LANES : (ch + 3) * LANES] = low
    for t in range(OWN_MAX // BAND):
        place = (iota((BAND, LANES), 0) + t * BAND).astype(F32)
        chosen = jnp.concatenate(
            [(place == key[g : g + 1, :]).astype(F32).astype(BF16) for g in range(rows)], 1
        )
        both = dot(chosen, rhs[...])
        owned_ref[t * BAND : (t + 1) * BAND, :] = both[:, : 2 * LANES] + both[:, 2 * LANES :]
    for c in copies:
        c.wait()


def finish(block_map, tile_owner):
    vmem = pl.BlockSpec(memory_space=pltpu.VMEM)
    return pl.pallas_call(
        finish_kernel,
        out_shape=(
            jax.ShapeDtypeStruct((OWN_MAX, 2 * LANES), F32),
            jax.ShapeDtypeStruct((BLOCK_TILES, 2 * LANES), F32),
        ),
        in_specs=[vmem, vmem],
        out_specs=(vmem, pl.BlockSpec(memory_space=pltpu.HBM)),
        scratch_shapes=[pltpu.VMEM((BLOCK_TILES, 4 * LANES), BF16), pltpu.SemaphoreType.DMA((2,))],
        compiler_params=pltpu.CompilerParams(vmem_limit_bytes=16 << 20),
        name="finish",
    )(block_map, tile_owner)


def shards(kernel, pressure, velocity, entry_slot, slot_tile, tile_owner):
    square = (ENTRIES // LANES, LANES)
    partial, keys, ids = project(
        kernel,
        pressure.reshape(square),
        velocity.reshape(square),
        entry_slot.reshape(square),
        slot_tile.reshape(SLOTS // LANES, LANES),
    )
    block_map = exchange(partial, keys, ids)
    return finish(block_map, tile_owner.reshape(-1, LANES))


def solution(mesh):
    in_specs = (
        P(("vol", "pix"), None),
        P(("vol", "pix")),
        P(("vol", "pix")),
        P(("vol", "pix"), None),
        P(("vol", "pix"), None),
        P(),
    )
    out_specs = (P(("vol", "pix"), None), P("vol", None))
    return jax.shard_map(shards, mesh=mesh, in_specs=in_specs, out_specs=out_specs, check_vma=False)
```

time: 74.8 us -> 64.7 us (0.86)
  Pallas kernels: 73.9 us -> 63.8 us
    pallas_call x1, Pallas kernels: 62.4 us -> 56.5 us  [exchange(): pl.pallas_call(exchange_kernel, out_shape=jax.ShapeDtypeStruct((2, BLOCK_...]
    pallas_call x1, Pallas kernels: 7.69 us -> 5.02 us  [project(): pl.pallas_call(project_kernel, out_shape=tuple((jax.ShapeDtypeStruct(*o)...]
    pallas_call x1, Pallas kernels: 3.86 us -> 2.32 us  [finish(): pl.pallas_call(finish_kernel, out_shape=(jax.ShapeDtypeStruct((OWN_MAX, 2...]
where the time goes in v3:
time: 64.7 us; the launch traced here: 64.5 us
  Pallas kernels  63.8 us (99%)
  between operations  0.66 us (1%)
    pallas_call x1, Pallas kernels, exchange(): pl.pallas_call(exchange_kernel, out_shape=jax.ShapeDtypeStruct((2, BLOCK_...  56.5 us
    pallas_call x1, Pallas kernels, project(): pl.pallas_call(project_kernel, out_shape=tuple((jax.ShapeDtypeStruct(*o)...  5.02 us
    pallas_call x1, Pallas kernels, finish(): pl.pallas_call(finish_kernel, out_shape=(jax.ShapeDtypeStruct((OWN_MAX, 2...  2.32 us

profile of v3, /device:TPU:1, one launch (start us, length us, event | category | flops | bytes accessed | tf_op | source)
XLA Modules:
  0.0 64.5 jit_solution(1374182828459481168)
XLA Ops:
  0.6 5.0 %project.1 = (bf16[1024,512]{1,0:T(8,128)(2,1)S(1)}, f32[128,128]{1,0:T(8,128)S(1)}, f32[16,128]{1,0:T(8,128)S(1)}) custom-call(bf16[16384,128]{1,0:T(8,128)(2,1)} %kernel_h.1, bf16[128,128]{1,0:T(8,128)(2,1)} %bitcast.7, bf16[128,128]{1,0:T(8,128)(2,1)} %bitcast.8, s32[128,128]{1,0:T(8,128)} %bitcast.6, s32[8,128]{1,0:T(8,128)} %bitcast.9), custom_call_target="tpu_custom_call" | custom-call | tf_op jit(solution)/shard_map/project/pallas_call | solution.py:156
  5.7 0.0 copy-start
  5.7 56.5 %exchange.1.map_ref = f32[2,2048,128]{2,1,0:T(8,128)S(1)} custom-call(bf16[1024,512]{1,0:T(8,128)(2,1)S(1)} %get-tuple-element.5.partial, f32[128,128]{1,0:T(8,128)S(1)} %get-tuple-element.6.keys, f32[16,128]{1,0:T(8,128)S(1)} %get-tuple-element.7.ids_ref), custom_call_target="tpu_custom_call" | custom-call | tf_op jit(solution)/shard_map/exchange/pallas_call | solution.py:391
  62.2 0.0 copy-done
  62.2 2.3 %finish.1 = (f32[512,256]{1,0:T(8,128)}, f32[2048,256]{1,0:T(8,128)}) custom-call(f32[2,2048,128]{2,1,0:T(8,128)S(1)} %exchange.1.map_ref, s32[256,128]{1,0:T(8,128)S(1)} %bitcast.5), custom_call_target="tpu_custom_call" | custom-call | tf_op jit(solution)/shard_map/finish/pallas_call | solution.py:453
Async XLA Ops:
  5.7 56.5 %copy-start = (s32[32768]{0:T(1024)S(1)}, s32[32768]{0:T(1024)}, u32[]{:S(2)}) copy-start(s32[32768]{0:T(1024)} %param.11) | copy-start | bytes 393220

commit v4 on v3

--- a/solution.py
+++ b/solution.py
@@ -45,7 +45,7 @@
 
 
 def project_kernel(
-    kernel_h, pressure_h, velocity_h, slot_h, tile_h, rhs_ref, key_ref, ids_ref,
+    kernel_h, pressure_h, velocity_h, slot_h, tile_h, rhs_ref, pick_ref, ids_ref,
     weights, pressure, velocity, slot_v, tile_v, slot_s, acc, sems, chunk_sems,
 ):
     steps = ENTRIES // STEP
@@ -82,12 +82,16 @@
     ones = jnp.ones((LANES, LANES), BF16)
     packed = match.astype(BF16)
     rank = dot(packed, before) + dot(dot(above, packed).astype(BF16), ones)
-    key_ref[...] = jnp.where(match > 0, rank, -1.0)
+    key = jnp.where(match > 0, rank, -1.0).astype(BF16)
     own = jnp.zeros((groups, LANES), F32)
     for v in range(N_VOL):
         own += match[v * groups : (v + 1) * groups] * rank[v * groups : (v + 1) * groups]
     place = iota((LANES, LANES), 0).astype(F32).astype(BF16)
     spread = jnp.concatenate([equal(place, own[g : g + 1].astype(BF16)) for g in range(groups)], 1)
+    for v in range(N_VOL):
+        for g in range(groups):
+            row = v * groups + g
+            pick_ref[v * CAP : (v + 1) * CAP, g * LANES : (g + 1) * LANES] = equal(place, key[row : row + 1])
     vols = iota((N_VOL, LANES), 0)
     upper, lower = (within // 64).astype(F32), (within % 64).astype(F32)
     table = []
@@ -132,17 +136,23 @@
         count = STEP // SPAN
         bases, lasts = [], []
         for i in range(count):
-            bases.append(pl.multiple_of((slot_s[top + i * per, 0] // 8) * 8, 8))
+            bases.append(pl.multiple_of(slot_s[top + i * per, 0] & -8, 8))
             lasts.append(slot_s[top + i * per + per - 1, LANES - 1])
         values = [products(i, bases[i]) for i in range(count)]
         for i in range(count):
             add(bases[i], values[i])
-        for i in range(count):
-
-            @pl.loop(1, (lasts[i] - bases[i]) // WINDOW + 1)
-            def _(w, i=i):
-                base = pl.multiple_of(bases[i] + w * WINDOW, 8)
-                add(base, products(i, base))
+        widest = lasts[0] - bases[0]
+        for i in range(1, count):
+            widest = jnp.maximum(widest, lasts[i] - bases[i])
+
+        @pl.when(widest >= WINDOW)
+        def _():
+            for i in range(count):
+
+                @pl.loop(1, (lasts[i] - bases[i]) // WINDOW + 1)
+                def _(w, i=i):
+                    base = pl.multiple_of(bases[i] + w * WINDOW, 8)
+                    add(base, products(i, base))
 
     for ch in range(2):
         high, low = halves(acc[ch, :SLOTS, :])
@@ -151,7 +161,7 @@
 
 
 def project(kernel, pressure, velocity, entry_slot, slot_tile):
-    outs = (((SLOTS, 4 * LANES), BF16), ((LANES, LANES), F32), ((N_VOL, LANES), F32))
+    outs = (((SLOTS, 4 * LANES), BF16), ((N_VOL * CAP, SLOTS), BF16), ((N_VOL, LANES), F32))
     square = (ENTRIES // LANES, LANES)
     return pl.pallas_call(
         project_kernel,
@@ -186,7 +196,7 @@
 
 
 def exchange_kernel(
-    partial, keys, ids_ref, out, send, recv, acc, other, parts, rhs, hot, pick,
+    partial, pick, ids_ref, out, send, recv, acc, other, parts, rhs, hot,
     p1s, p1r, d2s, d2r, rss, rsr, ags, agr, fws, fwr,
 ):
     vol = lax.axis_index("vol")
@@ -206,60 +216,59 @@
     for peer in peers:
         pl.semaphore_signal(barrier, inc=1, device_id=peer, device_id_type=MESH)
 
-    started = []
-
-    def copy(src, dst, s, r, peer):
-        c = pltpu.make_async_remote_copy(
+    def remote(src, dst, s, r, peer):
+        return pltpu.make_async_remote_copy(
             src_ref=src, dst_ref=dst, send_sem=s, recv_sem=r, device_id=peer, device_id_type=MESH
         )
+
+    def copy(src, dst, s, r, peer):
+        c = remote(src, dst, s, r, peer)
         c.start()
-        started.append(c)
         return c
 
     spans = ((0, FIRST), (FIRST, CAP))
     rows_of = (0, FIRST)
-    first = [[None] * N_VOL for _ in range(2)]
-
-    def launch(ch, k):
+    def launch(ch, n):
         begin, size = spans[ch]
-        to = vol_to(k)
-        first[ch][k] = copy(
-            send.at[k, pl.ds(begin, size)],
-            recv.at[k, pl.ds(begin, size)],
-            p1s.at[ch, k], p1r.at[ch, k], {"vol": to},
+        copy(
+            send.at[n, pl.ds(begin, size)],
+            recv.at[n, pl.ds(begin, size)],
+            p1s.at[0], p1r.at[ch, n // GROUP], {"vol": vol_to(ORDER[n])},
         )
 
-    place = iota((CAP, LANES), 0).astype(F32).astype(BF16)
-    groups = SLOTS // LANES
-
-    def batch(ch, n, ks):
-        here = slice(n * CAP, (n + len(ks)) * CAP)
-        if ch == 0:
-            for m, k in enumerate(ks):
-                key = keys[pl.ds(pl.multiple_of(vol_to(k) * groups, groups), groups), :]
-                pick[(n + m) * CAP : (n + m + 1) * CAP, :] = jnp.concatenate(
-                    [equal(place, key[g : g + 1, :].astype(BF16)) for g in range(groups)], 1
-                )
-                send[k, CAP:FIRST, :] = jnp.broadcast_to(ids_ref[pl.ds(vol_to(k), 1), :], (8, LANES))
-        both = dot(pick[here, :], partial[:, 2 * ch * LANES : 2 * (ch + 1) * LANES])
+    def arrived(ch, group):
+        begin, size = spans[ch]
+        low = max(group * GROUP, 1)
+        span = pl.ds(low, (group + 1) * GROUP - low)
+        span = recv.at[span, pl.ds(begin, size)]
+        remote(span, span, p1s.at[0], p1r.at[ch, group], partner).wait_recv()
+
+    def batch(ch, ns):
+        rows = []
+        for n in ns:
+            to = vol_to(ORDER[n])
+            rows.append(pick[pl.ds(pl.multiple_of(to * CAP, CAP), CAP), :])
+            if ch == 0:
+                send[n, CAP:FIRST, :] = jnp.broadcast_to(ids_ref[pl.ds(to, 1), :], (8, LANES))
+        both = dot(jnp.concatenate(rows, 0), partial[:, 2 * ch * LANES : 2 * (ch + 1) * LANES])
         total = both[:, :LANES] + both[:, LANES:]
-        for m, k in enumerate(ks):
-            send[k, rows_of[ch] : rows_of[ch] + CAP, :] = total[m * CAP : (m + 1) * CAP]
-
-    todo = ORDER[1:] + ORDER[:1]
+        for m, n in enumerate(ns):
+            send[n, rows_of[ch] : rows_of[ch] + CAP, :] = total[m * CAP : (m + 1) * CAP]
+
+    todo = tuple(range(1, N_VOL)) + (0,)
     waiting = []
     with jax.named_scope("messages"):
         for ch in range(2):
             for n in range(0, N_VOL, ROUND):
-                ks = todo[n : n + ROUND]
-                batch(ch, n, ks)
+                ns = todo[n : n + ROUND]
+                batch(ch, ns)
                 if ch == 0 and n == 0:
                     pl.semaphore_wait(barrier, len(peers))
-                for c, k in waiting:
-                    launch(c, k)
-                waiting = [(ch, k) for k in ks if k]
-        for c, k in waiting:
-            launch(c, k)
+                for c, m in waiting:
+                    launch(c, m)
+                waiting = [(ch, m) for m in ns if m]
+        for c, m in waiting:
+            launch(c, m)
 
     band = iota((BAND, LANES), 0).astype(F32).astype(BF16)
     mine = core * HALF
@@ -268,11 +277,10 @@
 
     def load(ch, group):
         ids = []
+        arrived(ch, group)
         for n in range(GROUP):
-            k = ORDER[group * GROUP + n]
+            k = group * GROUP + n
             source = recv if k else send
-            if k:
-                first[ch][k].wait_recv()
             ids.append(source[k, CAP : CAP + 1, :])
             high, low = halves(source[k, rows_of[ch] : rows_of[ch] + CAP, :])
             rhs[n * CAP : (n + 1) * CAP, :LANES] = high
@@ -319,7 +327,7 @@
             for s in range(SUBS):
                 at = pl.multiple_of(theirs + s * SUB, SUB)
                 copies.append(
-                    copy(acc.at[ch, pl.ds(at, SUB)], other.at[ch, s], d2s.at[ch, s], d2r.at[ch, s], partner)
+                    copy(acc.at[ch, pl.ds(at, SUB)], other.at[ch, s], d2s.at[0], d2r.at[ch, s], partner)
                 )
             tiles(ch, group, ids, mine, HALF // TALL)
         return copies
@@ -334,7 +342,7 @@
                 copies.append(
                     copy(
                         acc.at[ch, pl.ds(at, PIECE)], parts.at[ch, s, k - 1],
-                        rss.at[ch, s, k - 1], rsr.at[ch, s, k - 1], pix_to(k),
+                        rss.at[0], rsr.at[ch, s], pix_to(k),
                     )
                 )
         return copies
@@ -342,17 +350,16 @@
     def gather_start(ch, s, copies):
         with jax.named_scope(f"gather{ch}{s}"):
             here = pl.multiple_of(mine + s * SUB + x * PIECE, PIECE)
-            for c in copies:
-                c.wait_recv()
+            remote(parts.at[ch, s], parts.at[ch, s], rss.at[0], rsr.at[ch, s], partner).wait_recv()
             total = acc[ch, pl.ds(here, PIECE), :]
             for k in range(1, SIDE):
                 total += parts[ch, s, k - 1]
             out[ch, pl.ds(here, PIECE), :] = total
             block = out.at[ch, pl.ds(here, PIECE)]
             gathers = [
-                (k, copy(block, block, ags.at[ch, s, k - 1], agr.at[ch, s, k - 1], pix_to(k))) for k in (2, 1, 3)
+                (k, copy(block, block, ags.at[0], agr.at[ch, s, k - 1], pix_to(k))) for k in (2, 1, 3)
             ]
-        return gathers, [copy(block, block, fws.at[ch, s, 0], fwr.at[ch, s, 0], partner)]
+        return gathers, [copy(block, block, fws.at[0], fwr.at[ch], partner)]
 
     def forward(ch, s, started_gathers):
         gathers, sent = started_gathers
@@ -361,14 +368,14 @@
                 c.wait_recv()
                 at = pl.multiple_of(mine + s * SUB + lax.rem(x - k + SIDE, SIDE) * PIECE, PIECE)
                 block = out.at[ch, pl.ds(at, PIECE)]
-                sent.append(copy(block, block, fws.at[ch, s, k], fwr.at[ch, s, k], partner))
+                copy(block, block, fws.at[0], fwr.at[ch], partner)
         return sent
 
     for g in range(3):
         combine(0, g)
     s0 = combine_swap(0, 3)
+    r0 = [reduce_start(0, s, s0[s]) for s in range(SUBS)]
     combine(1, 0)
-    r0 = [reduce_start(0, s, s0[s]) for s in range(SUBS)]
     combine(1, 1)
     combine(1, 2)
     g0 = [gather_start(0, s, r0[s]) for s in range(SUBS)]
@@ -378,14 +385,20 @@
     g1 = [gather_start(1, s, r1[s]) for s in range(SUBS)]
     f1 = [forward(1, s, g1[s]) for s in range(SUBS)]
     with jax.named_scope("last"):
-        for f in f0 + f1:
-            for c in f:
-                c.wait_recv()
-        for c in started:
-            c.wait_send()
-
-
-def exchange(partial, keys, ids):
+        for ch in range(2):
+            block = out.at[ch, pl.ds(pl.multiple_of(theirs, HALF), HALF)]
+            remote(block, block, fws.at[0], fwr.at[ch], partner).wait_recv()
+        for whole, sem in (
+            (send.at[pl.ds(1, N_VOL - 1)], p1s),
+            (other, d2s),
+            (parts, rss),
+            (parts, ags),
+            (out.at[:, pl.ds(0, HALF)], fws),
+        ):
+            remote(whole, whole, sem.at[0], d2r.at[0, 0], partner).wait_send()
+
+
+def exchange(partial, pick, ids):
     vmem = pl.BlockSpec(memory_space=pltpu.VMEM)
     dma = pltpu.SemaphoreType.DMA
     return pl.pallas_call(
@@ -401,21 +414,20 @@
             pltpu.VMEM((2, SUBS, SIDE - 1, PIECE, LANES), F32),
             pltpu.VMEM((GROUP * CAP, 2 * LANES), BF16),
             pltpu.VMEM((BLOCK_TILES, N_VOL * CAP), BF16),
-            pltpu.VMEM((N_VOL * CAP, SLOTS), BF16),
-            dma((2, N_VOL)), dma((2, N_VOL)),
-            dma((2, SUBS)), dma((2, SUBS)),
-            dma((2, SUBS, SIDE - 1)), dma((2, SUBS, SIDE - 1)),
-            dma((2, SUBS, SIDE - 1)), dma((2, SUBS, SIDE - 1)),
-            dma((2, SUBS, SIDE)), dma((2, SUBS, SIDE)),
+            dma((1,)), dma((2, N_VOL // GROUP)),
+            dma((1,)), dma((2, SUBS)),
+            dma((1,)), dma((2, SUBS)),
+            dma((1,)), dma((2, SUBS, SIDE - 1)),
+            dma((1,)), dma((2,)),
         ],
         compiler_params=pltpu.CompilerParams(
             collective_id=0, has_side_effects=True, vmem_limit_bytes=32 << 20
         ),
         name="exchange",
-    )(partial, keys, ids)
-
-
-def finish_kernel(map_ref, owner_ref, owned_ref, shell_h, rhs, sems):
+    )(partial, pick, ids)
+
+
+def finish_kernel(map_ref, owner_ref, owned_h, shell_h, owned, rhs, sems):
     vol = lax.axis_index("vol")
     pix = lax.axis_index("pix")
     copies = []
@@ -437,13 +449,17 @@
         high, low = halves(map_ref[ch])
         rhs[:, ch * LANES : (ch + 1) * LANES] = high
         rhs[:, (ch + 2) * LANES : (ch + 3) * LANES] = low
+    place = iota((BAND, LANES), 0).astype(F32).astype(BF16)
     for t in range(OWN_MAX // BAND):
-        place = (iota((BAND, LANES), 0) + t * BAND).astype(F32)
-        chosen = jnp.concatenate(
-            [(place == key[g : g + 1, :]).astype(F32).astype(BF16) for g in range(rows)], 1
-        )
+        local = key - t * BAND
+        local = jnp.where((local >= 0) & (local < BAND), local, -1.0).astype(BF16)
+        chosen = jnp.concatenate([equal(place, local[g : g + 1]) for g in range(rows)], 1)
         both = dot(chosen, rhs[...])
-        owned_ref[t * BAND : (t + 1) * BAND, :] = both[:, : 2 * LANES] + both[:, 2 * LANES :]
+        here = pl.ds(t * BAND, BAND)
+        owned[here, :] = both[:, : 2 * LANES] + both[:, 2 * LANES :]
+        c = pltpu.make_async_copy(owned.at[here], owned_h.at[here], sems.at[2 + t])
+        c.start()
+        copies.append(c)
     for c in copies:
         c.wait()
 
@@ -457,8 +473,12 @@
             jax.ShapeDtypeStruct((BLOCK_TILES, 2 * LANES), F32),
         ),
         in_specs=[vmem, vmem],
-        out_specs=(vmem, pl.BlockSpec(memory_space=pltpu.HBM)),
-        scratch_shapes=[pltpu.VMEM((BLOCK_TILES, 4 * LANES), BF16), pltpu.SemaphoreType.DMA((2,))],
+        out_specs=(pl.BlockSpec(memory_space=pltpu.HBM),) * 2,
+        scratch_shapes=[
+            pltpu.VMEM((OWN_MAX, 2 * LANES), F32),
+            pltpu.VMEM((BLOCK_TILES, 4 * LANES), BF16),
+            pltpu.SemaphoreType.DMA((2 + OWN_MAX // BAND,)),
+        ],
         compiler_params=pltpu.CompilerParams(vmem_limit_bytes=16 << 20),
         name="finish",
     )(block_map, tile_owner)
@@ -466,14 +486,14 @@
 
 def shards(kernel, pressure, velocity, entry_slot, slot_tile, tile_owner):
     square = (ENTRIES // LANES, LANES)
-    partial, keys, ids = project(
+    partial, pick, ids = project(
         kernel,
         pressure.reshape(square),
         velocity.reshape(square),
         entry_slot.reshape(square),
         slot_tile.reshape(SLOTS // LANES, LANES),
     )
-    block_map = exchange(partial, keys, ids)
+    block_map = exchange(partial, pick, ids)
     return finish(block_map, tile_owner.reshape(-1, LANES))
 
 

time: 64.7 us -> 63.1 us (0.975)
  Pallas kernels: 63.8 us -> 62.4 us
    pallas_call x1, Pallas kernels: 56.5 us -> 55.3 us  [exchange(): pl.pallas_call(exchange_kernel, out_shape=jax.ShapeDtypeStruct((2, BLOCK_...]
where the time goes in v4:
time: 63.1 us; the launch traced here: 63 us
  Pallas kernels  62.4 us (99%)
  between operations  0.66 us (1%)
    pallas_call x1, Pallas kernels, exchange(): pl.pallas_call(exchange_kernel, out_shape=jax.ShapeDtypeStruct((2, BLOCK_...  55.3 us
    pallas_call x1, Pallas kernels, project(): pl.pallas_call(project_kernel, out_shape=tuple((jax.ShapeDtypeStruct(*o)...  4.77 us
    pallas_call x1, Pallas kernels, finish(): pl.pallas_call(finish_kernel, out_shape=(jax.ShapeDtypeStruct((OWN_MAX, 2...  2.31 us

profile of v4, /device:TPU:1, one launch (start us, length us, event | category | flops | bytes accessed | tf_op | source)
XLA Modules:
  0.0 63.0 jit_solution(4727403364545391816)
XLA Ops:
  0.6 4.8 %project.1 = (bf16[1024,512]{1,0:T(8,128)(2,1)S(1)}, bf16[2048,1024]{1,0:T(8,128)(2,1)S(1)}, f32[16,128]{1,0:T(8,128)S(1)}) custom-call(bf16[16384,128]{1,0:T(8,128)(2,1)} %kernel_h.1, bf16[128,128]{1,0:T(8,128)(2,1)} %bitcast.7, bf16[128,128]{1,0:T(8,128)(2,1)} %bitcast.8, s32[128,128]{1,0:T(8,128)} %bitcast.6, s32[8,128]{1,0:T(8,128)} %bitcast.9), custom_call_target="tpu_custom_call" | custom-call | tf_op jit(solution)/shard_map/project/pallas_call | solution.py:166
  5.4 0.0 copy-start
  5.4 55.3 %exchange.1.map_ref = f32[2,2048,128]{2,1,0:T(8,128)S(1)} custom-call(bf16[1024,512]{1,0:T(8,128)(2,1)S(1)} %get-tuple-element.5.partial, bf16[2048,1024]{1,0:T(8,128)(2,1)S(1)} %get-tuple-element.6.pick, f32[16,128]{1,0:T(8,128)S(1)} %get-tuple-element.7.ids_ref), custom_call_target="tpu_custom_call" | custom-call | tf_op jit(solution)/shard_map/exchange/pallas_call | solution.py:404
  60.7 0.0 copy-done
  60.7 2.3 %finish.1 = (f32[512,256]{1,0:T(8,128)}, f32[2048,256]{1,0:T(8,128)}) custom-call(f32[2,2048,128]{2,1,0:T(8,128)S(1)} %exchange.1.map_ref, s32[256,128]{1,0:T(8,128)S(1)} %bitcast.5), custom_call_target="tpu_custom_call" | custom-call | tf_op jit(solution)/shard_map/finish/pallas_call | solution.py:469
Async XLA Ops:
  5.4 55.3 %copy-start = (s32[32768]{0:T(1024)S(1)}, s32[32768]{0:T(1024)}, u32[]{:S(2)}) copy-start(s32[32768]{0:T(1024)} %param.11) | copy-start | bytes 393220

commit v5 on v4

--- a/solution.py
+++ b/solution.py
@@ -191,8 +191,8 @@
 PIECE = SUB // SIDE
 TALL = 1024
 BAND = 256
-ORDER = (0, 1, 4, 3, 12, 5, 15, 7, 13, 2, 8, 6, 9, 10, 14, 11)
-ROUND = 4
+ORDER = (0, 4, 12, 1, 3, 8, 2, 5, 7, 13, 15, 9, 11, 6, 14, 10)
+ROUND = 16
 
 
 def exchange_kernel(
@@ -226,7 +226,7 @@
         c.start()
         return c
 
-    spans = ((0, FIRST), (FIRST, CAP))
+    spans = ((0, CAP + 1), (FIRST, CAP))
     rows_of = (0, FIRST)
     def launch(ch, n):
         begin, size = spans[ch]
@@ -256,19 +256,18 @@
             send[n, rows_of[ch] : rows_of[ch] + CAP, :] = total[m * CAP : (m + 1) * CAP]
 
     todo = tuple(range(1, N_VOL)) + (0,)
-    waiting = []
     with jax.named_scope("messages"):
-        for ch in range(2):
-            for n in range(0, N_VOL, ROUND):
-                ns = todo[n : n + ROUND]
-                batch(ch, ns)
-                if ch == 0 and n == 0:
-                    pl.semaphore_wait(barrier, len(peers))
-                for c, m in waiting:
-                    launch(c, m)
-                waiting = [(ch, m) for m in ns if m]
-        for c, m in waiting:
-            launch(c, m)
+        for n in range(0, N_VOL, ROUND):
+            batch(0, todo[n : n + ROUND])
+        pl.semaphore_wait(barrier, len(peers))
+        for n in range(1, N_VOL):
+            launch(0, n)
+        for n in range(0, N_VOL, ROUND):
+            batch(1, todo[n : n + ROUND])
+
+    def launch_second():
+        for n in range(1, N_VOL):
+            launch(1, n)
 
     band = iota((BAND, LANES), 0).astype(F32).astype(BF16)
     mine = core * HALF
@@ -278,6 +277,8 @@
     def load(ch, group):
         ids = []
         arrived(ch, group)
+        if ch == 0 and group == 1:
+            launch_second()
         for n in range(GROUP):
             k = group * GROUP + n
             source = recv if k else send
@@ -389,7 +390,8 @@
             block = out.at[ch, pl.ds(pl.multiple_of(theirs, HALF), HALF)]
             remote(block, block, fws.at[0], fwr.at[ch], partner).wait_recv()
         for whole, sem in (
-            (send.at[pl.ds(1, N_VOL - 1)], p1s),
+            (send.at[pl.ds(1, N_VOL - 1), pl.ds(0, CAP + 1)], p1s),
+            (send.at[pl.ds(1, N_VOL - 1), pl.ds(FIRST, CAP)], p1s),
             (other, d2s),
             (parts, rss),
             (parts, ags),

time: 63.1 us -> 61 us (0.967)
  Pallas kernels: 62.4 us -> 60.2 us
    pallas_call x1, Pallas kernels: 55.3 us -> 53.1 us  [exchange(): pl.pallas_call(exchange_kernel, out_shape=jax.ShapeDtypeStruct((2, BLOCK_...]
where the time goes in v5:
time: 61 us; the launch traced here: 60.9 us
  Pallas kernels  60.2 us (99%)
  between operations  0.66 us (1%)
    pallas_call x1, Pallas kernels, exchange(): pl.pallas_call(exchange_kernel, out_shape=jax.ShapeDtypeStruct((2, BLOCK_...  53.1 us
    pallas_call x1, Pallas kernels, project(): pl.pallas_call(project_kernel, out_shape=tuple((jax.ShapeDtypeStruct(*o)...  4.77 us
    pallas_call x1, Pallas kernels, finish(): pl.pallas_call(finish_kernel, out_shape=(jax.ShapeDtypeStruct((OWN_MAX, 2...  2.3 us

profile of v5, /device:TPU:1, one launch (start us, length us, event | category | flops | bytes accessed | tf_op | source)
XLA Modules:
  0.0 60.9 jit_solution(2979811461446394650)
XLA Ops:
  0.6 4.8 %project.1 = (bf16[1024,512]{1,0:T(8,128)(2,1)S(1)}, bf16[2048,1024]{1,0:T(8,128)(2,1)S(1)}, f32[16,128]{1,0:T(8,128)S(1)}) custom-call(bf16[16384,128]{1,0:T(8,128)(2,1)} %kernel_h.1, bf16[128,128]{1,0:T(8,128)(2,1)} %bitcast.7, bf16[128,128]{1,0:T(8,128)(2,1)} %bitcast.8, s32[128,128]{1,0:T(8,128)} %bitcast.6, s32[8,128]{1,0:T(8,128)} %bitcast.9), custom_call_target="tpu_custom_call" | custom-call | tf_op jit(solution)/shard_map/project/pallas_call | solution.py:166
  5.4 0.0 copy-start
  5.4 53.1 %exchange.1.map_ref = f32[2,2048,128]{2,1,0:T(8,128)S(1)} custom-call(bf16[1024,512]{1,0:T(8,128)(2,1)S(1)} %get-tuple-element.5.partial, bf16[2048,1024]{1,0:T(8,128)(2,1)S(1)} %get-tuple-element.6.pick, f32[16,128]{1,0:T(8,128)S(1)} %get-tuple-element.7.ids_ref), custom_call_target="tpu_custom_call" | custom-call | tf_op jit(solution)/shard_map/exchange/pallas_call | solution.py:406
  58.6 0.0 copy-done
  58.6 2.3 %finish.1 = (f32[512,256]{1,0:T(8,128)}, f32[2048,256]{1,0:T(8,128)}) custom-call(f32[2,2048,128]{2,1,0:T(8,128)S(1)} %exchange.1.map_ref, s32[256,128]{1,0:T(8,128)S(1)} %bitcast.5), custom_call_target="tpu_custom_call" | custom-call | tf_op jit(solution)/shard_map/finish/pallas_call | solution.py:471
Async XLA Ops:
  5.4 53.2 %copy-start = (s32[32768]{0:T(1024)S(1)}, s32[32768]{0:T(1024)}, u32[]{:S(2)}) copy-start(s32[32768]{0:T(1024)} %param.11) | copy-start | bytes 393220

commit v6 on v5

--- a/solution.py
+++ b/solution.py
@@ -20,7 +20,7 @@
 CAP = 128
 OWN_MAX = 512
 
-STEP = 2048
+STEP = 8192
 SPAN = 256
 WINDOW = 32
 MSG = 2 * CAP + 8
@@ -196,7 +196,7 @@
 
 
 def exchange_kernel(
-    partial, pick, ids_ref, out, send, recv, acc, other, parts, rhs, hot,
+    partial, pick, ids_ref, owner_ref, out, own0, own_hot, send, recv, acc, other, parts, rhs, hot, split,
     p1s, p1r, d2s, d2r, rss, rsr, ags, agr, fws, fwr,
 ):
     vol = lax.axis_index("vol")
@@ -372,23 +372,57 @@
                 copy(block, block, fws.at[0], fwr.at[ch], partner)
         return sent
 
-    for g in range(3):
-        combine(0, g)
+    def settled(ch):
+        block = out.at[ch, pl.ds(pl.multiple_of(theirs, HALF), HALF)]
+        remote(block, block, fws.at[0], fwr.at[ch], partner).wait_recv()
+
+    def owned_places():
+        with jax.named_scope("places"):
+            rows = BLOCK_TILES // LANES
+            owner = owner_ref[pl.ds(pl.multiple_of(vol * rows, rows), rows), :]
+            match = (owner == pix).astype(F32)
+            packed = match.astype(BF16)
+            before = (iota((LANES, LANES), 0) < iota((LANES, LANES), 1)).astype(F32).astype(BF16)
+            above = (iota((rows, rows), 1) < iota((rows, rows), 0)).astype(F32).astype(BF16)
+            ones = jnp.ones((LANES, LANES), BF16)
+            rank = dot(packed, before) + dot(dot(above, packed).astype(BF16), ones)
+            key = jnp.where(match > 0, rank, -1.0)
+            for t in range(OWN_MAX // BAND):
+                local = key - t * BAND
+                local = jnp.where((local >= 0) & (local < BAND), local, -1.0).astype(BF16)
+                for g in range(rows):
+                    own_hot[t * BAND : (t + 1) * BAND, g * LANES : (g + 1) * LANES] = equal(band, local[g : g + 1])
+
+    def owned_first():
+        with jax.named_scope("owned"):
+            settled(0)
+            high, low = halves(out[0])
+            split[:, :LANES] = high
+            split[:, LANES:] = low
+            both = dot(own_hot[...], split[...])
+            own0[...] = both[:, :LANES] + both[:, LANES:]
+
+    subs = range(SUBS)
+    combine(0, 0)
+    owned_places()
+    combine(0, 1)
+    combine(0, 2)
     s0 = combine_swap(0, 3)
-    r0 = [reduce_start(0, s, s0[s]) for s in range(SUBS)]
+    r0 = [reduce_start(0, s, s0[s]) for s in subs]
     combine(1, 0)
     combine(1, 1)
+    g0 = [gather_start(0, 0, r0[0])]
     combine(1, 2)
-    g0 = [gather_start(0, s, r0[s]) for s in range(SUBS)]
+    g0.append(gather_start(0, 1, r0[1]))
     s1 = combine_swap(1, 3)
-    r1 = [reduce_start(1, s, s1[s]) for s in range(SUBS)]
-    f0 = [forward(0, s, g0[s]) for s in range(SUBS)]
-    g1 = [gather_start(1, s, r1[s]) for s in range(SUBS)]
-    f1 = [forward(1, s, g1[s]) for s in range(SUBS)]
+    r1 = [reduce_start(1, s, s1[s]) for s in subs]
+    f0 = [forward(0, s, g0[s]) for s in subs]
+    g1 = [gather_start(1, 0, r1[0])]
+    owned_first()
+    g1.append(gather_start(1, 1, r1[1]))
+    f1 = [forward(1, s, g1[s]) for s in subs]
     with jax.named_scope("last"):
-        for ch in range(2):
-            block = out.at[ch, pl.ds(pl.multiple_of(theirs, HALF), HALF)]
-            remote(block, block, fws.at[0], fwr.at[ch], partner).wait_recv()
+        settled(1)
         for whole, sem in (
             (send.at[pl.ds(1, N_VOL - 1), pl.ds(0, CAP + 1)], p1s),
             (send.at[pl.ds(1, N_VOL - 1), pl.ds(FIRST, CAP)], p1s),
@@ -400,14 +434,18 @@
             remote(whole, whole, sem.at[0], d2r.at[0, 0], partner).wait_send()
 
 
-def exchange(partial, pick, ids):
+def exchange(partial, pick, ids, tile_owner):
     vmem = pl.BlockSpec(memory_space=pltpu.VMEM)
     dma = pltpu.SemaphoreType.DMA
     return pl.pallas_call(
         exchange_kernel,
-        out_shape=jax.ShapeDtypeStruct((2, BLOCK_TILES, LANES), F32),
-        in_specs=[vmem] * 3,
-        out_specs=vmem,
+        out_shape=(
+            jax.ShapeDtypeStruct((2, BLOCK_TILES, LANES), F32),
+            jax.ShapeDtypeStruct((OWN_MAX, LANES), F32),
+            jax.ShapeDtypeStruct((OWN_MAX, BLOCK_TILES), BF16),
+        ),
+        in_specs=[vmem] * 4,
+        out_specs=(vmem,) * 3,
         scratch_shapes=[
             pltpu.VMEM((N_VOL, MSG, LANES), F32),
             pltpu.VMEM((N_VOL, MSG, LANES), F32),
@@ -416,6 +454,7 @@
             pltpu.VMEM((2, SUBS, SIDE - 1, PIECE, LANES), F32),
             pltpu.VMEM((GROUP * CAP, 2 * LANES), BF16),
             pltpu.VMEM((BLOCK_TILES, N_VOL * CAP), BF16),
+            pltpu.VMEM((BLOCK_TILES, 2 * LANES), BF16),
             dma((1,)), dma((2, N_VOL // GROUP)),
             dma((1,)), dma((2, SUBS)),
             dma((1,)), dma((2, SUBS)),
@@ -426,47 +465,32 @@
             collective_id=0, has_side_effects=True, vmem_limit_bytes=32 << 20
         ),
         name="exchange",
-    )(partial, pick, ids)
-
-
-def finish_kernel(map_ref, owner_ref, owned_h, shell_h, owned, rhs, sems):
-    vol = lax.axis_index("vol")
-    pix = lax.axis_index("pix")
-    copies = []
-    for ch in range(2):
-        c = pltpu.make_async_copy(
-            map_ref.at[ch], shell_h.at[:, pl.ds(ch * LANES, LANES)], sems.at[ch]
-        )
+    )(partial, pick, ids, tile_owner)
+
+
+def finish_kernel(map_ref, own0, own_hot, owned_h, shell_h, owned, rhs, sems):
+    def put(source, target, n):
+        c = pltpu.make_async_copy(source, target, sems.at[n])
         c.start()
-        copies.append(c)
-    rows = BLOCK_TILES // LANES
-    owner = owner_ref[pl.ds(pl.multiple_of(vol * rows, rows), rows), :]
-    match = (owner == pix).astype(F32).astype(BF16)
-    before = (iota((LANES, LANES), 0) < iota((LANES, LANES), 1)).astype(F32).astype(BF16)
-    above = (iota((rows, rows), 1) < iota((rows, rows), 0)).astype(F32).astype(BF16)
-    ones = jnp.ones((LANES, LANES), BF16)
-    rank = dot(match, before) + dot(dot(above, match).astype(BF16), ones)
-    key = jnp.where(match.astype(F32) > 0, rank, -1.0)
-    for ch in range(2):
-        high, low = halves(map_ref[ch])
-        rhs[:, ch * LANES : (ch + 1) * LANES] = high
-        rhs[:, (ch + 2) * LANES : (ch + 3) * LANES] = low
-    place = iota((BAND, LANES), 0).astype(F32).astype(BF16)
-    for t in range(OWN_MAX // BAND):
-        local = key - t * BAND
-        local = jnp.where((local >= 0) & (local < BAND), local, -1.0).astype(BF16)
-        chosen = jnp.concatenate([equal(place, local[g : g + 1]) for g in range(rows)], 1)
-        both = dot(chosen, rhs[...])
-        here = pl.ds(t * BAND, BAND)
-        owned[here, :] = both[:, : 2 * LANES] + both[:, 2 * LANES :]
-        c = pltpu.make_async_copy(owned.at[here], owned_h.at[here], sems.at[2 + t])
-        c.start()
-        copies.append(c)
+        return c
+
+    left, right = pl.ds(0, LANES), pl.ds(LANES, LANES)
+    copies = [
+        put(map_ref.at[1], shell_h.at[:, right], 0),
+        put(map_ref.at[0], shell_h.at[:, left], 1),
+        put(own0, owned_h.at[:, left], 2),
+    ]
+    high, low = halves(map_ref[1])
+    rhs[:, :LANES] = high
+    rhs[:, LANES:] = low
+    both = dot(own_hot[...], rhs[...])
+    owned[...] = both[:, :LANES] + both[:, LANES:]
+    copies.append(put(owned, owned_h.at[:, right], 3))
     for c in copies:
         c.wait()
 
 
-def finish(block_map, tile_owner):
+def finish(block_map, own0, own_hot):
     vmem = pl.BlockSpec(memory_space=pltpu.VMEM)
     return pl.pallas_call(
         finish_kernel,
@@ -474,16 +498,16 @@
             jax.ShapeDtypeStruct((OWN_MAX, 2 * LANES), F32),
             jax.ShapeDtypeStruct((BLOCK_TILES, 2 * LANES), F32),
         ),
-        in_specs=[vmem, vmem],
+        in_specs=[vmem] * 3,
         out_specs=(pl.BlockSpec(memory_space=pltpu.HBM),) * 2,
         scratch_shapes=[
-            pltpu.VMEM((OWN_MAX, 2 * LANES), F32),
-            pltpu.VMEM((BLOCK_TILES, 4 * LANES), BF16),
-            pltpu.SemaphoreType.DMA((2 + OWN_MAX // BAND,)),
+            pltpu.VMEM((OWN_MAX, LANES), F32),
+            pltpu.VMEM((BLOCK_TILES, 2 * LANES), BF16),
+            pltpu.SemaphoreType.DMA((4,)),
         ],
         compiler_params=pltpu.CompilerParams(vmem_limit_bytes=16 << 20),
         name="finish",
-    )(block_map, tile_owner)
+    )(block_map, own0, own_hot)
 
 
 def shards(kernel, pressure, velocity, entry_slot, slot_tile, tile_owner):
@@ -495,8 +519,8 @@
         entry_slot.reshape(square),
         slot_tile.reshape(SLOTS // LANES, LANES),
     )
-    block_map = exchange(partial, pick, ids)
-    return finish(block_map, tile_owner.reshape(-1, LANES))
+    block_map, own0, own_hot = exchange(partial, pick, ids, tile_owner.reshape(-1, LANES))
+    return finish(block_map, own0, own_hot)
 
 
 def solution(mesh):

time: 61 us -> 59.1 us (0.969)
  Pallas kernels: 60.2 us -> 58.1 us
    pallas_call x1, Pallas kernels: 4.77 us -> 3.45 us  [project(): pl.pallas_call(project_kernel, out_shape=tuple((jax.ShapeDtypeStruct(*o)...]
    pallas_call x1, Pallas kernels: 2.3 us -> 1.55 us  [finish(): pl.pallas_call(finish_kernel, out_shape=(jax.ShapeDtypeStruct((OWN_MAX, 2...]
where the time goes in v6:
time: 59.1 us; the launch traced here: 59 us
  Pallas kernels  58.1 us (98%)
  between operations  0.82 us (1%)
    pallas_call x1, Pallas kernels, exchange(): pl.pallas_call(exchange_kernel, out_shape=(jax.ShapeDtypeStruct((2, BLOCK...  53.1 us
    pallas_call x1, Pallas kernels, project(): pl.pallas_call(project_kernel, out_shape=tuple((jax.ShapeDtypeStruct(*o)...  3.45 us
    pallas_call x1, Pallas kernels, finish(): pl.pallas_call(finish_kernel, out_shape=(jax.ShapeDtypeStruct((OWN_MAX, 2...  1.55 us

profile of v6, /device:TPU:1, one launch (start us, length us, event | category | flops | bytes accessed | tf_op | source)
XLA Modules:
  0.0 59.0 jit_solution(10213957389535612655)
XLA Ops:
  0.6 0.0 copy-start
  0.6 3.4 %project.1 = (bf16[1024,512]{1,0:T(8,128)(2,1)S(1)}, bf16[2048,1024]{1,0:T(8,128)(2,1)S(1)}, f32[16,128]{1,0:T(8,128)S(1)}) custom-call(bf16[16384,128]{1,0:T(8,128)(2,1)} %kernel_h.1, bf16[128,128]{1,0:T(8,128)(2,1)} %bitcast.7, bf16[128,128]{1,0:T(8,128)(2,1)} %bitcast.8, s32[128,128]{1,0:T(8,128)} %bitcast.6, s32[8,128]{1,0:T(8,128)} %bitcast.9), custom_call_target="tpu_custom_call" | custom-call | tf_op jit(solution)/shard_map/project/pallas_call | solution.py:166
  4.1 0.0 copy-done
  4.1 53.1 %exchange.1 = (f32[2,2048,128]{2,1,0:T(8,128)S(1)}, f32[512,128]{1,0:T(8,128)S(1)}, bf16[512,2048]{1,0:T(8,128)(2,1)S(1)}) custom-call(bf16[1024,512]{1,0:T(8,128)(2,1)S(1)} %get-tuple-element.8.partial, bf16[2048,1024]{1,0:T(8,128)(2,1)S(1)} %get-tuple-element.9.pick, f32[16,128]{1,0:T(8,128)S(1)} %get-tuple-element.10.ids_ref, s32[256,128]{1,0:T(8,128)S(1)} %bitcast.5), custom_call_target="tpu_custom_call" | custom-call | tf_op jit(solution)/shard_map/exchange/pallas_call | solution.py:440
  57.2 1.6 %finish.1 = (f32[512,256]{1,0:T(8,128)}, f32[2048,256]{1,0:T(8,128)}) custom-call(f32[2,2048,128]{2,1,0:T(8,128)S(1)} %get-tuple-element.11.map_ref, f32[512,128]{1,0:T(8,128)S(1)} %get-tuple-element.12.own0, bf16[512,2048]{1,0:T(8,128)(2,1)S(1)} %get-tuple-element.13.own_hot), custom_call_target="tpu_custom_call" | custom-call | tf_op jit(solution)/shard_map/finish/pallas_call | solution.py:495
Async XLA Ops:
  0.6 3.5 %copy-start = (s32[32768]{0:T(1024)S(1)}, s32[32768]{0:T(1024)}, u32[]{:S(2)}) copy-start(s32[32768]{0:T(1024)} %param.11) | copy-start | bytes 393220

commit v7 on v6

--- a/solution.py
+++ b/solution.py
@@ -22,7 +22,7 @@
 
 STEP = 8192
 SPAN = 256
-WINDOW = 32
+WINDOW = 40
 MSG = 2 * CAP + 8
 FIRST = CAP + 8
 
@@ -191,7 +191,7 @@
 PIECE = SUB // SIDE
 TALL = 1024
 BAND = 256
-ORDER = (0, 4, 12, 1, 3, 8, 2, 5, 7, 13, 15, 9, 11, 6, 14, 10)
+ORDER = (0, 4, 1, 12, 3, 8, 2, 5, 15, 13, 7, 9, 6, 11, 14, 10)
 ROUND = 16
 
 

time: 59.1 us -> 59 us (level)
  no operation moved by 1% of the time
where the time goes in v7:
time: 59 us; the launch traced here: 58.9 us
  Pallas kernels  58.1 us (98%)
  between operations  0.82 us (1%)
    pallas_call x1, Pallas kernels, exchange(): pl.pallas_call(exchange_kernel, out_shape=(jax.ShapeDtypeStruct((2, BLOCK...  53 us
    pallas_call x1, Pallas kernels, project(): pl.pallas_call(project_kernel, out_shape=tuple((jax.ShapeDtypeStruct(*o)...  3.51 us
    pallas_call x1, Pallas kernels, finish(): pl.pallas_call(finish_kernel, out_shape=(jax.ShapeDtypeStruct((OWN_MAX, 2...  1.56 us

profile of v7, /device:TPU:1, one launch (start us, length us, event | category | flops | bytes accessed | tf_op | source)
XLA Modules:
  0.0 58.9 jit_solution(12932334615575666353)
XLA Ops:
  0.6 0.0 copy-start
  0.6 3.5 %project.1 = (bf16[1024,512]{1,0:T(8,128)(2,1)S(1)}, bf16[2048,1024]{1,0:T(8,128)(2,1)S(1)}, f32[16,128]{1,0:T(8,128)S(1)}) custom-call(bf16[16384,128]{1,0:T(8,128)(2,1)} %kernel_h.1, bf16[128,128]{1,0:T(8,128)(2,1)} %bitcast.7, bf16[128,128]{1,0:T(8,128)(2,1)} %bitcast.8, s32[128,128]{1,0:T(8,128)} %bitcast.6, s32[8,128]{1,0:T(8,128)} %bitcast.9), custom_call_target="tpu_custom_call" | custom-call | tf_op jit(solution)/shard_map/project/pallas_call | solution.py:166
  4.2 0.0 copy-done
  4.2 53.0 %exchange.1 = (f32[2,2048,128]{2,1,0:T(8,128)S(1)}, f32[512,128]{1,0:T(8,128)S(1)}, bf16[512,2048]{1,0:T(8,128)(2,1)S(1)}) custom-call(bf16[1024,512]{1,0:T(8,128)(2,1)S(1)} %get-tuple-element.8.partial, bf16[2048,1024]{1,0:T(8,128)(2,1)S(1)} %get-tuple-element.9.pick, f32[16,128]{1,0:T(8,128)S(1)} %get-tuple-element.10.ids_ref, s32[256,128]{1,0:T(8,128)S(1)} %bitcast.5), custom_call_target="tpu_custom_call" | custom-call | tf_op jit(solution)/shard_map/exchange/pallas_call | solution.py:440
  57.2 1.6 %finish.1 = (f32[512,256]{1,0:T(8,128)}, f32[2048,256]{1,0:T(8,128)}) custom-call(f32[2,2048,128]{2,1,0:T(8,128)S(1)} %get-tuple-element.11.map_ref, f32[512,128]{1,0:T(8,128)S(1)} %get-tuple-element.12.own0, bf16[512,2048]{1,0:T(8,128)(2,1)S(1)} %get-tuple-element.13.own_hot), custom_call_target="tpu_custom_call" | custom-call | tf_op jit(solution)/shard_map/finish/pallas_call | solution.py:495
Async XLA Ops:
  0.6 3.5 %copy-start = (s32[32768]{0:T(1024)S(1)}, s32[32768]{0:T(1024)}, u32[]{:S(2)}) copy-start(s32[32768]{0:T(1024)} %param.11) | copy-start | bytes 393220

commit v8 on v7

--- a/solution.py
+++ b/solution.py
@@ -184,7 +184,8 @@
     )(*(pltpu.with_memory_space_constraint(a, pltpu.HBM) for a in (kernel, pressure, velocity, entry_slot, slot_tile)))
 
 
-GROUP = 4
+GROUPS = ((0, 5), (5, 4), (9, 4), (13, 3))
+LARGEST = max(size for _, size in GROUPS)
 SUBS = 2
 HALF = BLOCK_TILES // 2
 SUB = HALF // SUBS
@@ -195,6 +196,10 @@
 ROUND = 16
 
 
+def group_of(n):
+    return [start <= n < start + count for start, count in GROUPS].index(True)
+
+
 def exchange_kernel(
     partial, pick, ids_ref, owner_ref, out, own0, own_hot, send, recv, acc, other, parts, rhs, hot, split,
     p1s, p1r, d2s, d2r, rss, rsr, ags, agr, fws, fwr,
@@ -233,13 +238,14 @@
         copy(
             send.at[n, pl.ds(begin, size)],
             recv.at[n, pl.ds(begin, size)],
-            p1s.at[0], p1r.at[ch, n // GROUP], {"vol": vol_to(ORDER[n])},
+            p1s.at[0], p1r.at[ch, group_of(n)], {"vol": vol_to(ORDER[n])},
         )
 
     def arrived(ch, group):
         begin, size = spans[ch]
-        low = max(group * GROUP, 1)
-        span = pl.ds(low, (group + 1) * GROUP - low)
+        start, count = GROUPS[group]
+        low = max(start, 1)
+        span = pl.ds(low, start + count - low)
         span = recv.at[span, pl.ds(begin, size)]
         remote(span, span, p1s.at[0], p1r.at[ch, group], partner).wait_recv()
 
@@ -272,15 +278,14 @@
     band = iota((BAND, LANES), 0).astype(F32).astype(BF16)
     mine = core * HALF
     theirs = HALF - mine
-    turn = GROUP * CAP
 
     def load(ch, group):
         ids = []
         arrived(ch, group)
         if ch == 0 and group == 1:
             launch_second()
-        for n in range(GROUP):
-            k = group * GROUP + n
+        for n in range(GROUPS[group][1]):
+            k = GROUPS[group][0] + n
             source = recv if k else send
             ids.append(source[k, CAP : CAP + 1, :])
             high, low = halves(source[k, rows_of[ch] : rows_of[ch] + CAP, :])
@@ -289,7 +294,8 @@
         return ids
 
     def tiles(ch, group, ids, begin, count):
-        columns = slice(group * turn, (group + 1) * turn)
+        start, count_in = GROUPS[group]
+        columns = slice(start * CAP, (start + count_in) * CAP)
 
         def one(t):
             at = pl.multiple_of(begin + t * TALL, TALL)
@@ -302,7 +308,7 @@
                         local = jnp.where((local >= 0) & (local < BAND), local, -1.0)
                         pieces.append(equal(band, local.astype(BF16)))
                     hot[pl.ds(low, BAND), columns] = jnp.concatenate(pieces, 1)
-            both = dot(hot[pl.ds(at, TALL), columns], rhs[...])
+            both = dot(hot[pl.ds(at, TALL), columns], rhs[: count_in * CAP, :])
             total = both[:, :LANES] + both[:, LANES:]
             if group:
                 total += acc[ch, pl.ds(at, TALL), :]
@@ -452,10 +458,10 @@
             pltpu.VMEM((2, BLOCK_TILES, LANES), F32),
             pltpu.VMEM((2, SUBS, SUB, LANES), F32),
             pltpu.VMEM((2, SUBS, SIDE - 1, PIECE, LANES), F32),
-            pltpu.VMEM((GROUP * CAP, 2 * LANES), BF16),
+            pltpu.VMEM((LARGEST * CAP, 2 * LANES), BF16),
             pltpu.VMEM((BLOCK_TILES, N_VOL * CAP), BF16),
             pltpu.VMEM((BLOCK_TILES, 2 * LANES), BF16),
-            dma((1,)), dma((2, N_VOL // GROUP)),
+            dma((1,)), dma((2, len(GROUPS))),
             dma((1,)), dma((2, SUBS)),
             dma((1,)), dma((2, SUBS)),
             dma((1,)), dma((2, SUBS, SIDE - 1)),

time: 59 us -> 59.8 us (1.014)
  Pallas kernels: 58.1 us -> 58.8 us
    pallas_call x1, Pallas kernels: 53 us -> 53.8 us  [exchange(): pl.pallas_call(exchange_kernel, out_shape=(jax.ShapeDtypeStruct((2, BLOCK...]
where the time goes in v8:
time: 59.8 us; the launch traced here: 59.7 us
  Pallas kernels  58.8 us (98%)
  between operations  0.82 us (1%)
    pallas_call x1, Pallas kernels, exchange(): pl.pallas_call(exchange_kernel, out_shape=(jax.ShapeDtypeStruct((2, BLOCK...  53.8 us
    pallas_call x1, Pallas kernels, project(): pl.pallas_call(project_kernel, out_shape=tuple((jax.ShapeDtypeStruct(*o)...  3.53 us
    pallas_call x1, Pallas kernels, finish(): pl.pallas_call(finish_kernel, out_shape=(jax.ShapeDtypeStruct((OWN_MAX, 2...  1.55 us

profile of v8, /device:TPU:1, one launch (start us, length us, event | category | flops | bytes accessed | tf_op | source)
XLA Modules:
  0.0 59.7 jit_solution(17766732755054466083)
XLA Ops:
  0.6 0.0 copy-start
  0.6 3.5 %project.1 = (bf16[1024,512]{1,0:T(8,128)(2,1)S(1)}, bf16[2048,1024]{1,0:T(8,128)(2,1)S(1)}, f32[16,128]{1,0:T(8,128)S(1)}) custom-call(bf16[16384,128]{1,0:T(8,128)(2,1)} %kernel_h.1, bf16[128,128]{1,0:T(8,128)(2,1)} %bitcast.7, bf16[128,128]{1,0:T(8,128)(2,1)} %bitcast.8, s32[128,128]{1,0:T(8,128)} %bitcast.6, s32[8,128]{1,0:T(8,128)} %bitcast.9), custom_call_target="tpu_custom_call" | custom-call | tf_op jit(solution)/shard_map/project/pallas_call | solution.py:166
  4.2 0.0 copy-done
  4.2 53.8 %exchange.1 = (f32[2,2048,128]{2,1,0:T(8,128)S(1)}, f32[512,128]{1,0:T(8,128)S(1)}, bf16[512,2048]{1,0:T(8,128)(2,1)S(1)}) custom-call(bf16[1024,512]{1,0:T(8,128)(2,1)S(1)} %get-tuple-element.8.partial, bf16[2048,1024]{1,0:T(8,128)(2,1)S(1)} %get-tuple-element.9.pick, f32[16,128]{1,0:T(8,128)S(1)} %get-tuple-element.10.ids_ref, s32[256,128]{1,0:T(8,128)S(1)} %bitcast.5), custom_call_target="tpu_custom_call" | custom-call | tf_op jit(solution)/shard_map/exchange/pallas_call | solution.py:446
  58.0 1.6 %finish.1 = (f32[512,256]{1,0:T(8,128)}, f32[2048,256]{1,0:T(8,128)}) custom-call(f32[2,2048,128]{2,1,0:T(8,128)S(1)} %get-tuple-element.11.map_ref, f32[512,128]{1,0:T(8,128)S(1)} %get-tuple-element.12.own0, bf16[512,2048]{1,0:T(8,128)(2,1)S(1)} %get-tuple-element.13.own_hot), custom_call_target="tpu_custom_call" | custom-call | tf_op jit(solution)/shard_map/finish/pallas_call | solution.py:501
Async XLA Ops:
  0.6 3.5 %copy-start = (s32[32768]{0:T(1024)S(1)}, s32[32768]{0:T(1024)}, u32[]{:S(2)}) copy-start(s32[32768]{0:T(1024)} %param.11) | copy-start | bytes 393220
